TPU v7x, 256 devices: a whole 4x4x8 slice. The times are simulated.
256 devices in a mesh: dp: 8 (over x, core), vocab: 32 (over z, y).
Axes of the slice: x: 4, y: 4, z: 8, core: 2. Of those that a mesh axis runs over, the one named last changes fastest.
Arguments:
- hidden: bfloat16 [1024, 8192], P(('dp', 'vocab')), may hold values from -350 to 350
- lm_head: bfloat16 [8192, 128256], P(None, ('dp', 'vocab')), may hold values from -0.0625 to 0.0625
- targets: int32 [1024], P(('dp', 'vocab')), may hold values from 0 to 128255
- segment: int32 [1024], P(('dp', 'vocab')), may hold values from 0 to 256, as said below
- pad_mask: int32 [1024], P(('dp', 'vocab')), may hold values from 0 to 1, as said below
- seq_bench: int32 [257], replicated, may hold values from 0 to 7
Outputs:
- token_nll: float32 [1024], P(('dp', 'vocab'))
- bench_total: float32 [8], replicated
- bench_count: float32 [8], replicated
Inputs may be any that keep to these rules, and one draw needn't show every extreme that they name: `segment`: sequence numbers never fall along the pack; each aligned block of 4 tokens holds exactly one place inside it where the number rises by one, and the number does not change between one block's last token and the next block's first. `pad_mask`: the last token of each aligned block of 4 tokens is real.
All inputs are finite; a program needn't handle non-finite values.
Results may differ from a plain program's by a relative error of at most 0.0003.
Values may be sent and summed in bfloat16 or wider, within the bound.
A program may use at most 128 MiB of HBM per device.

v0:
```python
from functools import partial
import functools

import jax
import jax.numpy as jnp
from jax import lax
from jax.sharding import Mesh
from jax.sharding import PartitionSpec as P

NBENCH = 8
DP_VOCAB = ("dp_0", "dp_1", "vocab_0", "vocab_1")
VOCAB = ("vocab_0", "vocab_1")
DP = ("dp_0", "dp_1")


def laid_out(pieces, dim):
    pieces = jnp.moveaxis(pieces, 0, dim)
    shape = pieces.shape
    return pieces.reshape(*shape[:dim], shape[dim] * shape[dim + 1], *shape[dim + 2 :])


def gather_in_order(value, axes, sequence):
    pieces = value
    for k in sequence:
        pieces = lax.all_gather(pieces, axes[k])
    done = sequence[::-1]
    back = [done.index(k) for k in range(len(axes))]
    pieces = pieces.transpose(*back, *range(len(axes), pieces.ndim))
    return pieces.reshape(-1, *value.shape)


def gathered_by_axis(value, axes, sequence, dim):
    return laid_out(gather_in_order(value, axes, sequence), dim)


def whole_of(value, axes, dim):
    out = value
    for number in range(len(axes) - 1, -1, -1):
        out = lax.all_gather(out, axes[number], axis=dim, tiled=True)
    return out


def gathered_once(value, axis):
    leaves = jax.tree.leaves(value)
    sequence = sorted(range(len(leaves)), key=lambda k: -leaves[k].size)
    width = (1, *leaves[sequence[0]].shape)[-1]
    lines = [
        jnp.pad(leaves[k].reshape(-1), (0, -leaves[k].size % width)).reshape(-1, width)
        for k in sequence
    ]
    both, at, found = (lax.all_gather(jnp.concatenate(lines), axis), 0, {})
    for k, line in zip(sequence, lines):
        share = both[:, at : at + len(line)].reshape(len(both), -1)
        found[k] = share[:, : leaves[k].size].reshape(-1, *leaves[k].shape)
        at += len(line)
    numbers = iter(range(len(leaves)))
    return jax.tree.map(lambda _: found[next(numbers)], value)


def merged_by_axis(value, axes, combine):
    for axis in axes:
        pieces = gathered_once(value, axis)
        value = jax.tree.map(lambda part: part[0], pieces)
        for k in range(1, lax.axis_size(axis)):
            value = combine(value, jax.tree.map(lambda part: part[k], pieces))
    return value


def from_behind(value, axis, steps):
    count = lax.axis_size(axis)
    leading, last = (max(0, -steps), min(count, count - steps))
    return lax.ppermute(value, axis, [(source, source + steps) for source in range(leading, last)])


def one_axis_at_a_time(value, axes):
    return functools.reduce(lax.psum, axes, value)


def shard_stats(piece, start, lm_head, all_targets, col_start):
    logits = jnp.dot(piece, lm_head, preferred_element_type=jnp.float32)
    row_top = jnp.max(logits, axis=1)
    expsum = jnp.sum(jnp.exp(logits - row_top[:, None]), axis=1)
    wanted = all_targets - col_start
    columns = lax.broadcasted_iota(jnp.int32, logits.shape, 1)
    picked = jnp.sum(jnp.where(columns == wanted[:, None], logits, 0.0), axis=1)
    return jnp.stack([row_top, expsum, picked], axis=0)


def merge_rows(first, second):
    top = jnp.maximum(first[0], second[0])
    total = first[1] * jnp.exp(first[0] - top) + second[1] * jnp.exp(second[0] - top)
    return (top, total, first[2] + second[2])


def body(hidden, lm_head, targets, segment, pad_mask, seq_bench):
    tok_dev = hidden.shape[0]
    voc_dev = lm_head.shape[1]
    own_index = lax.axis_index(DP_VOCAB)
    col_start = own_index * voc_dev
    row_start = own_index * tok_dev
    all_targets = gathered_by_axis(targets, DP_VOCAB, (0, 2, 3, 1), 0)
    per_piece = partial(shard_stats, lm_head=lm_head, all_targets=all_targets, col_start=col_start)
    group_rows = whole_of(hidden, VOCAB, 0)
    stats = per_piece(lax.all_gather(group_rows, DP, axis=0, tiled=True), jnp.int32(0))
    top_all, total_all, picked_all = merged_by_axis(
        (stats[0], stats[1], stats[2]), DP_VOCAB, merge_rows
    )
    top = lax.dynamic_slice_in_dim(top_all, row_start, tok_dev, 0)
    total = lax.dynamic_slice_in_dim(total_all, row_start, tok_dev, 0)
    picked = lax.dynamic_slice_in_dim(picked_all, row_start, tok_dev, 0)
    token_nll = top + jnp.log(total) - picked
    next_first = from_behind(segment[:1] + 1, DP_VOCAB, -1)
    following = jnp.concatenate([segment[1:] + 1, next_first])
    keep = (pad_mask * (segment + 1 == following).astype(jnp.int32)).astype(jnp.float32)
    seq_count = seq_bench.shape[0]
    seq_hot = segment[:, None] == lax.broadcasted_iota(jnp.int32, (1, seq_count), 1)
    bench_of = jnp.sum(jnp.where(seq_hot, seq_bench[None, :], 0), axis=1)
    bench_hot = (bench_of[:, None] == lax.broadcasted_iota(jnp.int32, (1, NBENCH), 1)).astype(
        jnp.float32
    )
    weighted = keep * token_nll
    bench_total, bench_count = (
        one_axis_at_a_time(jnp.sum(bench_hot * weighted[:, None], axis=0), DP_VOCAB),
        one_axis_at_a_time(jnp.sum(bench_hot * keep[:, None], axis=0), DP_VOCAB),
    )
    return (token_nll, bench_total, bench_count)


def solution(mesh):
    split = Mesh(mesh.devices.reshape(4, 2, 8, 4), ("dp_0", "dp_1", "vocab_0", "vocab_1"))
    return jax.shard_map(
        body,
        mesh=split,
        in_specs=(P(DP_VOCAB, None), P(None, DP_VOCAB), P(DP_VOCAB), P(DP_VOCAB), P(DP_VOCAB), P()),
        out_specs=(P(DP_VOCAB), P(), P()),
        check_vma=False,
    )
```

profile of v0, /device:TPU:1, one launch (start us, length us, event | category | flops | bytes accessed | tf_op | source)
XLA Modules:
  0.0 261.5 jit_solution(8159874351671681301)
XLA Ops:
  7.3 11.4 %all-gather.8 = bf16[4,4,8192]{2,1,0:T(4,128)(2,1)S(1)} all-gather(bf16[1,4,8192]{2,1,0:T(4,128)(2,1)} %bitcast.295), channel_id=1, replica_groups=mesh['dp_0'=4,'dp_1'=2,'vocab_0'=8,'vocab_1'=4] {'vocab_1'}, dimensions={0}, use_global_device_ids=true | all-gather | bytes 327680 | tf_op jit(solution)/shard_map/all_gather | solution.py:39
  18.7 0.8 reshape.920
  19.5 0.0 all-gather.19.cloned.1.call-start
  19.5 41.4 %all-gather.17.cloned.1.call-done = bf16[128,8192]{1,0:T(8,128)(2,1)} async-done(((bf16[16,8192]{1,0:T(8,128)(2,1)}), bf16[128,8192]{1,0:T(8,128)(2,1)}) %all-gather.17.cloned.1.call-update) | async-done | bytes 2097168 | tf_op jit(solution)/shard_map/all_gather | solution.py:39
  61.0 11.3 %collective-permute-start = (s32[1]{0:T(128)}, s32[1]{0:T(128)}, u32[]{:S(2)}, u32[]{:S(2)}) collective-permute-start(s32[1]{0:T(128)} %add.335), channel_id=1, source_target_pairs={{1,0},{2,1},{3,2},{4,3},{5,4},{6,5},{7,6},{8,7},{9,8},{10,9},{11,1... | collective-permute-start | bytes 20 | tf_op jit(solution)/shard_map/ppermute | solution.py:72
  72.4 0.6 dynamic-slice.1
  73.6 0.2 dynamic-update-slice
  73.9 6.8 %all-reduce = s32[16]{0:T(128)S(1)} all-reduce(s32[16]{0:T(128)S(1)} %dynamic-update-slice), channel_id=2, replica_groups=mesh['dp_0'=4,'dp_1'=2,'vocab_0'=8,'vocab_1'=4] {'dp_0'}, use_global_device_ids=true, to_apply=%add | all-reduce | flops 16 | bytes 128
  80.7 0.1 reshape.921
  80.8 18.1 %all-gather.9 = s32[8,4,4]{2,1,0:T(4,128)S(1)} all-gather(s32[1,4,4]{2,1,0:T(4,128)S(1)} %reshape.921), channel_id=3, replica_groups=mesh['dp_0'=4,'dp_1'=2,'vocab_0'=8,'vocab_1'=4] {'vocab_0'}, dimensions={0}, use_global_device_ids=true | all-gather | bytes 576 | tf_op jit(solution)/shard_map/all_gather | solution.py:25
  98.9 10.2 %all-gather.2 = s32[32,4,4]{2,1,0:T(4,128)S(1)} all-gather(s32[8,4,4]{2,1,0:T(4,128)S(1)} %all-gather.9), channel_id=4, replica_groups=mesh['dp_0'=4,'dp_1'=2,'vocab_0'=8,'vocab_1'=4] {'vocab_1'}, dimensions={0}, use_global_device_ids=true | all-gather | bytes 2560 | tf_op jit(solution)/shard_map/all_gather | solution.py:25
  109.1 0.2 copy.14
  109.2 9.9 %all-gather.3 = s32[8,8,4,4]{1,3,2,0:T(4,128)S(1)} all-gather(s32[4,8,4,4]{1,3,2,0:T(4,128)S(1)} %copy.14), channel_id=5, replica_groups=mesh['dp_0'=4,'dp_1'=2,'vocab_0'=8,'vocab_1'=4] {'dp_1'}, dimensions={0}, use_global_device_ids=true | all-gather | bytes 6144 | tf_op jit(solution)/shard_map/all_gather | solution.py:25
  119.1 0.3 copy.16
  119.4 0.2 sub.270
  119.5 0.2 select_reduce_fusion.1
  119.7 0.1 slice_add_fusion.11
  119.8 33.6 %all-gather.19.cloned.1.call-done = bf16[1024,8192]{1,0:T(8,128)(2,1)} async-done(((bf16[128,8192]{1,0:T(8,128)(2,1)}), bf16[1024,8192]{1,0:T(8,128)(2,1)}) %all-gather.19.cloned.1.call-update) | async-done | bytes 16777232 | tf_op jit(solution)/shard_map/all_gather | solution.py:104
  153.4 14.3 %fusion.61 = (f32[1024]{0:T(1024)S(1)}, f32[1024,501]{0,1:T(8,128)S(1)}) fusion(bf16[1024,8192]{1,0:T(8,128)(2,1)} %all-gather.19.cloned.1.call-done, bf16[8192,501]{0,1:T(8,128)(2,1)} %param.7), kind=kOutput, calls=%fused_computation.115 | convolution fusion | flops 8405897216 | bytes 27041792 | tf_op jit(solution)/shard_map/dot_general | solution.py:80
  167.8 0.5 exponential_reduce_fusion
  168.3 9.0 %all-gather.10 = f32[4,3,1024]{2,1,0:T(4,128)S(1)} all-gather(f32[1,3,1024]{2,1,0:T(4,128)S(1)} %maximum_bitcast_fusion), channel_id=6, replica_groups=mesh['dp_0'=4,'dp_1'=2,'vocab_0'=8,'vocab_1'=4] {'dp_0'}, dimensions={0}, use_global_device_ids=true | all-gather | bytes 61440 | tf_op jit(solution)/shard_map/all_gather | solution.py:51
  177.3 0.1 fusion.28
  177.4 4.6 %all-gather.11 = f32[2,3,1024]{2,1,0:T(4,128)S(1)} all-gather(f32[1,3,1024]{2,1,0:T(4,128)S(1)} %maximum_bitcast_fusion.1), channel_id=7, replica_groups=mesh['dp_0'=4,'dp_1'=2,'vocab_0'=8,'vocab_1'=4] {'dp_1'}, dimensions={0}, use_global_device_ids=true | all-gather | bytes 36864 | tf_op jit(solution)/shard_map/all_gather | solution.py:51
  182.1 19.7 %all-gather.12 = f32[8,3,1024]{2,1,0:T(4,128)S(1)} all-gather(f32[1,3,1024]{2,1,0:T(4,128)S(1)} %maximum_bitcast_fusion.2), channel_id=8, replica_groups=mesh['dp_0'=4,'dp_1'=2,'vocab_0'=8,'vocab_1'=4] {'vocab_0'}, dimensions={0}, use_global_device_ids=true | all-gather | bytes 110592 | tf_op jit(solution)/shard_map/all_gather | solution.py:51
  201.9 0.1 fusion.2
  202.0 9.6 %all-gather.13 = f32[4,3,1024]{2,1,0:T(4,128)S(1)} all-gather(f32[1,3,1024]{2,1,0:T(4,128)S(1)} %maximum_bitcast_fusion.3), channel_id=9, replica_groups=mesh['dp_0'=4,'dp_1'=2,'vocab_0'=8,'vocab_1'=4] {'vocab_1'}, dimensions={0}, use_global_device_ids=true | all-gather | bytes 61440 | tf_op jit(solution)/shard_map/all_gather | solution.py:51
  211.7 1.2 fusion.53
  212.9 0.1 select_reduce_fusion.2
  213.0 7.6 %all-reduce.3 = (f32[8]{0:T(128)S(1)}, f32[8]{0:T(128)S(1)}) all-reduce(f32[8]{0:T(128)S(1)} %get-tuple-element.6, f32[8]{0:T(128)S(1)} %get-tuple-element.5), channel_id=1, replica_groups=mesh['dp_0'=4,'dp_1'=2,'vocab_0'=8,'vocab_1'=4] {'dp_0'}, use_global_device_ids=true, to_apply=%region_5.6 | all-reduce | flops 16 | bytes 128 | tf_op jit(solution)/shard_map/psum | solution.py:76
  220.6 13.0 %all-reduce.4 = (f32[8]{0:T(128)S(1)}, f32[8]{0:T(128)S(1)}) all-reduce(f32[8]{0:T(128)S(1)} %get-tuple-element.11, f32[8]{0:T(128)S(1)} %get-tuple-element.12), channel_id=1, replica_groups=mesh['dp_0'=4,'dp_1'=2,'vocab_0'=8,'vocab_1'=4] {'dp_1'}, use_global_device_ids=true, to_apply=%region_6.7 | all-reduce | flops 16 | bytes 128 | tf_op jit(solution)/shard_map/psum | solution.py:76
  233.6 12.5 %all-reduce.1 = (f32[8]{0:T(128)S(1)}, f32[8]{0:T(128)S(1)}) all-reduce(f32[8]{0:T(128)S(1)} %get-tuple-element.13, f32[8]{0:T(128)S(1)} %get-tuple-element.14), channel_id=1, replica_groups=mesh['dp_0'=4,'dp_1'=2,'vocab_0'=8,'vocab_1'=4] {'vocab_0'}, use_global_device_ids=true, to_apply=%region_7.8 | all-reduce | flops 16 | bytes 128 | tf_op jit(solution)/shard_map/psum | solution.py:76
  246.1 8.6 %all-reduce.2 = (f32[8]{0:T(128)}, f32[8]{0:T(128)}) all-reduce(f32[8]{0:T(128)S(1)} %get-tuple-element.7, f32[8]{0:T(128)S(1)} %get-tuple-element.8), channel_id=1, replica_groups=mesh['dp_0'=4,'dp_1'=2,'vocab_0'=8,'vocab_1'=4] {'vocab_1'}, use_global_device_ids=true, to_apply=%region_8.9 | all-reduce | flops 16 | bytes 128 | tf_op jit(solution)/shard_map/psum | solution.py:76
  (27 shorter events, 0.3 us)
Async XLA Ops:
  7.2 65.2 %copy-start.4 = (u32[256]{0:T(256)S(1)}, u32[256]{0:T(256)}, u32[]{:S(2)}) copy-start(u32[256]{0:T(256)} %constant.51) | copy-start | bytes 3076
  7.2 53.8 %copy-start = (s32[4]{0:T(128)S(1)}, s32[4]{0:T(128)}, u32[]{:S(2)}) copy-start(s32[4]{0:T(128)} %param.9) | copy-start | bytes 52
  7.2 66.4 %copy-start.3 = (s32[4]{0:T(128)S(1)}, s32[4]{0:T(128)}, u32[]{:S(2)}) copy-start(s32[4]{0:T(128)} %param.8) | copy-start | bytes 52
  7.2 112.3 %copy-start.1 = (s32[257]{0:T(512)S(1)}, s32[257]{0:T(512)}, u32[]{:S(2)}) copy-start(s32[257]{0:T(512)} %param.11) | copy-start | bytes 3088
  7.2 53.8 %all-gather.17.cloned.1.call-start = ((), (), s32[]{:S(2)}) async-start(), calls=%async_computation | async-start | bytes 2359296 | tf_op jit(solution)/shard_map/all_gather | solution.py:39
  19.5 134.0 %all-gather.19.cloned.1.call-start = ((), (), s32[]{:S(2)}) async-start(), calls=%async_computation.1 | async-start | bytes 18874368 | tf_op jit(solution)/shard_map/all_gather | solution.py:104
  61.0 150.6 %collective-permute-start = (s32[1]{0:T(128)}, s32[1]{0:T(128)}, u32[]{:S(2)}, u32[]{:S(2)}) collective-permute-start(s32[1]{0:T(128)} %add.335), channel_id=1, source_target_pairs={{1,0},{2,1},{3,2},{4,3},{5,4},{6,5},{7,6},{8,7},{9,8},{10,9},{11,1... | collective-permute-start | bytes 20 | tf_op jit(solution)/shard_map/ppermute | solution.py:72
  167.8 43.9 %copy-start.2 = (s32[4]{0:T(128)S(1)}, s32[4]{0:T(128)}, u32[]{:S(2)}) copy-start(s32[4]{0:T(128)} %param.10) | copy-start | bytes 52
Sparse Core Ops, SparseCore 0:
  19.6 41.3 all-gather.16
  62.8 90.5 all-gather.18
where the time goes:
time: 265 us; the launch traced here: 261 us
  blocking collectives  141 us (53%)
  waiting for transfers between devices  75.1 us (28%)
  between operations  14.9 us (6%)
  matrix products  14.3 us (5%)
  starting transfers between devices  11.4 us (4%)
    all_gather x4, blocking collectives, gathered_once(): both, at, found = (lax.all_gather(jnp.concatenate(lines), axis), 0, {})  42.9 us
    psum x4, blocking collectives, one_axis_at_a_time(): return functools.reduce(lax.psum, axes, value)  41.7 us
    all_gather x1, waiting for transfers between devices, whole_of(): out = lax.all_gather(out, axes[number], axis=dim, tiled=True)  41.4 us
    all_gather x3, blocking collectives, gather_in_order(): pieces = lax.all_gather(pieces, axes[k])  38.1 us
    all_gather x1, waiting for transfers between devices, body(): lax.all_gather(group_rows, DP, axis=0, tiled=True)  33.6 us
    dot_general x1, matrix products, shard_stats(): logits = jnp.dot(piece, lm_head, preferred_element_type=jnp.float32)  14.3 us
    all_gather x1, blocking collectives, whole_of(): out = lax.all_gather(out, axes[number], axis=dim, tiled=True)  11.4 us
    ppermute x1, starting transfers between devices, from_behind(): lax.ppermute(value, axis, [(source, source + steps) for source in range(l...  11.3 us
  transfers between devices with their start and end apart: 3, of which 2 were waited for; matrix products, arithmetic and copies ran while one was open for 7% of the time, Pallas kernels for 0%

commit v1 on v0

v1 whole, which is shorter than its diff:
```python
import functools

import jax
import jax.numpy as jnp
from jax import lax
from jax.experimental import pallas as pl
from jax.experimental.pallas import tpu as pltpu
from jax.sharding import Mesh
from jax.sharding import PartitionSpec as P

NBENCH = 8
AXES = ("dp_0", "dp_1", "vocab_0", "vocab_1")
NA, NB, NZ = 4, 4, 8
PIECES = 8
LAG = 6
GROUP = NA * NB * NZ
DIST = (0, NZ - 1, 1, NZ - 2, 2, NZ - 3, 3, 4)
MESH = pl.DeviceIdType.MESH
F32 = jnp.float32


def kernel(
    hidden, lm_head, targets, segment, pad_mask, seq_bench,
    nll_out, total_out, count_out,
    abuf, rows32, gath, wbuf, acc, tcol, info, stat, last, nllbuf,
    lsem, wlsem, wsend, wrecv, asend, arecv, zsend, zrecv,
    bsend, brecv, fsend, frecv, isend, irecv, ssend, srecv, csend, crecv,
):
    x, c = lax.axis_index("dp_0"), lax.axis_index("dp_1")
    z, y = lax.axis_index("vocab_0"), lax.axis_index("vocab_1")
    a = y * (1 - c) + x * c
    b = x * (1 - c) + y * c
    kp = abuf.shape[3]
    voc = lm_head.shape[1]

    def dev(a_, b_, z_, c_=None):
        if c_ is None:
            return (b_ * (1 - c) + a_ * c, c, z_, a_ * (1 - c) + b_ * c)
        return (x, c_, z, y)

    def rdma(src, dst, ssem, rsem, to):
        return pltpu.make_async_remote_copy(
            src_ref=src, dst_ref=dst, send_sem=ssem, recv_sem=rsem,
            device_id=to, device_id_type=MESH,
        )

    def a_at(k):
        return lax.rem(a + k, NA)

    def b_at(k):
        return lax.rem(b + k, NB)

    def z_at(k):
        return lax.rem(z + k, NZ)

    partner = dev(a, b, z, 1 - c)

    def own_hidden(p):
        cols = pl.ds(pl.multiple_of(p * kp, kp), kp)
        return pltpu.make_async_copy(hidden.at[:, cols], abuf.at[p, a], lsem.at[p])

    def own_weights(p):
        rows = pl.ds(pl.multiple_of(p * kp, kp), kp)
        return pltpu.make_async_copy(lm_head.at[rows, :], wbuf.at[0, rows, :], wlsem.at[p])

    def swap_weights(p):
        rows = pl.ds(pl.multiple_of(p * kp, kp), kp)
        return rdma(lm_head.at[rows, :], wbuf.at[1, rows, :], wsend, wrecv.at[p], partner)

    def loop(n, body):
        lax.fori_loop(0, n, lambda i, _: (body(i), 0)[1], 0)

    loop(PIECES, lambda p: own_hidden(p).start())

    barrier = pltpu.get_barrier_semaphore()
    peers = (
        [dev(a_at(k), b, z) for k in range(1, NA)]
        + [dev(a, b_at(k), z) for k in range(1, NB)]
        + [dev(a, b, z_at(k)) for k in range(1, NZ)]
        + [partner]
    )
    for peer in peers:
        pl.semaphore_signal(barrier, inc=1, device_id=peer, device_id_type=MESH)

    row = lax.broadcasted_iota(jnp.int32, (8, 128), 0)
    lane = lax.broadcasted_iota(jnp.int32, (8, 128), 1)
    base = z * (NA * 4) + a * 4
    own = jnp.zeros((8, 128), jnp.int32)
    whole_last = (x == NA - 1) & (c == 1) & (z == NZ - 1) & (y == NB - 1)
    for t in range(4):
        seg = segment[t]
        if t < 3:
            kept = (pad_mask[t] == 1) & (seg == segment[t + 1])
        else:
            kept = (pad_mask[t] == 1) & jnp.logical_not(whole_last)
        code = jnp.where(kept, seq_bench[seg], NBENCH)
        own = jnp.where((row == b) & (lane == base + t), targets[t], own)
        own = jnp.where((row == b + 4) & (lane == base + t), code, own)
    own = own.astype(F32)

    loop(acc.shape[1] // 64, lambda i: zero_rows(acc, i))

    pl.semaphore_wait(barrier, len(peers))

    def a_copy(p, k):
        return rdma(abuf.at[p, a], abuf.at[p, a], asend, arecv.at[p, k - 1], dev(a_at(k), b, z))

    def a_start(p):
        own_hidden(p).wait()
        for k in range(1, NA):
            a_copy(p, k).start()

    loop(PIECES, a_start)
    loop(PIECES, lambda p: own_weights(p).start())
    loop(PIECES, lambda p: swap_weights(p).start())

    def stage(buf, at, n, me, ssem, rsem, to, value):
        buf[at + me] = value
        for k in range(1, n):
            rdma(buf.at[at + me], buf.at[at + me], ssem.at[at + k], rsem.at[at + k], to(k)).start()

    def stage_wait(buf, at, n, me, ssem, rsem, to):
        for k in range(1, n):
            rdma(buf.at[at + me], buf.at[at + me], ssem.at[at + k], rsem.at[at + k], to(k)).wait()

    def to_a(k):
        return dev(a_at(k), b, z)

    def to_b(k):
        return dev(a, b_at(k), z)

    def to_z(k):
        return dev(a, b, z_at(k))

    sa, sb, sz = (0, NA, a, ), (NA, NB, b), (NA + NB, NZ, z)

    def added(buf, at, n):
        total = buf[at]
        for k in range(1, n):
            total = total + buf[at + k]
        return total

    stage(info, *sa, isend, irecv, to_a, own)

    def block(p, b_, z_):
        return gath.at[p, b_, z_]

    def z_copy(p, k, sem, up):
        zi = z_at(k)
        return rdma(block(p, b, zi), block(p, b, zi), zsend, zrecv.at[p, sem], dev(a, b, z_at(up)))

    def b_copy(p, j, way):
        zi = z_at(DIST[j])
        return rdma(
            block(p, b, zi), block(p, b, zi), bsend, brecv.at[p, way, j],
            dev(a, b_at(1 if way == 0 else NB - 1), z),
        )

    def f_copy(p, j):
        zi = z_at(DIST[j])
        come, go = (NB - 1, 1) if j % 2 == 0 else (1, NB - 1)
        return rdma(
            block(p, b_at(come), zi), block(p, b_at(come), zi), fsend, frecv.at[p, j],
            dev(a, b_at(go), z),
        )

    def b_both(p, j):
        b_copy(p, j, 0).start()
        b_copy(p, j, 1).start()

    def step_0(p):
        for k in range(1, NA):
            a_copy(p, k).wait_recv()
        for k in range(NA):
            rows32[4 * k : 4 * k + 4, :] = abuf[p, k].astype(F32)
        gath[p, b, z] = rows32[...].astype(jnp.bfloat16)
        z_copy(p, 0, 0, 1).start()
        z_copy(p, 0, 1, NZ - 1).start()
        b_both(p, 0)

    def step(p, s):
        z_copy(p, NZ - s, 2 * s - 2, 1).wait_recv()
        if s < 3:
            z_copy(p, NZ - s, 2 * s, 1).start()
        z_copy(p, s, 2 * s - 1, NZ - 1).wait_recv()
        if s < 3:
            z_copy(p, s, 2 * s + 1, NZ - 1).start()
        else:
            odd = lax.rem(p, 2)
            z_copy(p, 5 + 6 * odd, 6, 1 + 6 * odd).start()
        b_both(p, 2 * s - 1)
        b_both(p, 2 * s)

    def step_4(p):
        z_copy(p, 4, 6, 1).wait_recv()
        b_both(p, 7)

    def forward(p, s):
        for j in ((0,), (1, 2), (3, 4), (5, 6), (7,))[s]:
            b_copy(p, j, j % 2).wait_recv()
            f_copy(p, j).start()

    def multiply(p):
        for j in range(8):
            b_copy(p, j, 1 - j % 2).wait_recv()
            f_copy(p, j).wait_recv()
        own_weights(p).wait()
        swap_weights(p).wait_recv()
        rows = pl.ds(pl.multiple_of(p * kp, kp), kp)
        for w in range(2):
            lhs = gath[p].reshape(acc.shape[1], kp)
            acc[w] += jnp.dot(lhs, wbuf[w, rows, :], preferred_element_type=F32)

    def at_piece(tick, lag, fn):
        p = tick - lag

        @pl.when((p >= 0) & (p < PIECES))
        def _():
            fn(p)

    eye = lax.broadcasted_iota(jnp.int32, (128, 128), 0) == lax.broadcasted_iota(
        jnp.int32, (128, 128), 1
    )

    def ticks(tick):
        at_piece(tick, 0, step_0)
        for s in range(1, 4):
            at_piece(tick, s, functools.partial(step, s=s))
        at_piece(tick, 4, step_4)
        for s in range(5):
            at_piece(tick, s + 1, functools.partial(forward, s=s))
        at_piece(tick, LAG, multiply)

        @pl.when(tick == 2)
        def _():
            stage_wait(info, *sa, isend, irecv, to_a)
            stage(info, *sb, isend, irecv, to_b, added(info, 0, NA))

        @pl.when(tick == 4)
        def _():
            stage_wait(info, *sb, isend, irecv, to_b)
            stage(info, *sz, isend, irecv, to_z, added(info, NA, NB))

        @pl.when(tick == 6)
        def _():
            stage_wait(info, *sz, isend, irecv, to_z)
            every = added(info, NA + NB, NZ)
            info[0] = every
            for k in range(4):
                wide = jnp.where(eye, jnp.broadcast_to(every[k : k + 1, :], (128, 128)), 0.0)
                tcol[k * 128 : (k + 1) * 128, :] = jnp.sum(wide, axis=1, keepdims=True)

    loop(PIECES + LAG, ticks)

    index = ((x * 2 + c) * NZ + z) * NB + y
    other = ((x * 2 + 1 - c) * NZ + z) * NB + y
    lanes = lax.broadcasted_iota(jnp.int32, (128, voc), 1)
    cols = [(lanes + i * voc).astype(F32) for i in (index, other)]

    def statistics(k):
        rows = pl.ds(pl.multiple_of(k * 128, 128), 128)
        own_l, other_l = acc[0, rows, :], acc[1, rows, :]
        wanted = tcol[rows, :]
        top = jnp.maximum(
            jnp.max(own_l, axis=1, keepdims=True), jnp.max(other_l, axis=1, keepdims=True)
        )
        total = jnp.sum(jnp.exp(own_l - top), axis=1, keepdims=True) + jnp.sum(
            jnp.exp(other_l - top), axis=1, keepdims=True
        )
        picked = jnp.sum(
            jnp.where(cols[0] == wanted, own_l, 0.0), axis=1, keepdims=True
        ) + jnp.sum(jnp.where(cols[1] == wanted, other_l, 0.0), axis=1, keepdims=True)
        lse = top + jnp.log(total)
        for at, value in ((0, lse), (4, picked)):
            wide = jnp.where(eye, jnp.broadcast_to(value, (128, 128)), 0.0)
            nllbuf[pl.ds(at + k, 1), :] = jnp.sum(wide, axis=0, keepdims=True)

    loop(4, statistics)

    def merged(buf, at, n):
        parts = [buf[at + k] for k in range(n)]
        top = functools.reduce(jnp.maximum, parts)
        total = functools.reduce(jnp.add, [jnp.exp(part - top) for part in parts])
        picked = functools.reduce(jnp.add, parts)
        return jnp.where(row < 4, top + jnp.log(total), picked)

    stage(stat, *sa, ssend, srecv, to_a, nllbuf[...])
    stage_wait(stat, *sa, ssend, srecv, to_a)
    stage(stat, *sb, ssend, srecv, to_b, merged(stat, 0, NA))
    stage_wait(stat, *sb, ssend, srecv, to_b)
    stage(stat, *sz, ssend, srecv, to_z, merged(stat, NA, NB))
    stage_wait(stat, *sz, ssend, srecv, to_z)
    both = merged(stat, NA + NB, NZ)
    nll = both[0:4, :] - both[4:8, :]

    codes = info[0][4:8, :]
    last_t, last_c = jnp.zeros((8, 128), F32), jnp.zeros((8, 128), F32)
    for j in range(NBENCH):
        hit = codes == float(j)
        part_t = jnp.sum(jnp.where(hit, nll, 0.0), axis=0, keepdims=True)
        part_c = jnp.sum(jnp.where(hit, 1.0, 0.0), axis=0, keepdims=True)
        last_t = jnp.where(row == j, part_t, last_t)
        last_c = jnp.where(row == j, part_c, last_c)
    last[c, 0:8, :] = last_t
    last[c, 8:16, :] = last_c
    swap = rdma(last.at[c], last.at[c], csend, crecv, partner)
    swap.start()

    nllbuf[0:4, :] = nll
    mine = nllbuf[pl.ds(b, 1), :]
    rolled = pltpu.roll(jnp.broadcast_to(mine, (8, 128)), lax.rem(128 - base, 128), 1)
    nll_out[...] = rolled[0:1, 0:4]

    rdma(abuf.at[:, 0:3], abuf.at[:, 0:3], asend, arecv.at[0, 0], partner).wait_send()
    rdma(wbuf.at[1], wbuf.at[1], wsend, wrecv.at[0], partner).wait_send()
    rdma(gath.at[:, 0, 0:7], gath.at[:, 0, 0:7], zsend, zrecv.at[0, 0], partner).wait_send()
    rdma(gath.at[:, 0:2], gath.at[:, 0:2], bsend, brecv.at[0, 0, 0], partner).wait_send()
    rdma(gath.at[:, 0], gath.at[:, 0], fsend, frecv.at[0, 0], partner).wait_send()

    swap.wait()
    sums = jnp.sum(last[0] + last[1], axis=1, keepdims=True)
    small = lax.broadcasted_iota(jnp.int32, (8, 8), 0) == lax.broadcasted_iota(jnp.int32, (8, 8), 1)
    for out, at in ((total_out, 0), (count_out, 8)):
        wide = jnp.where(small, jnp.broadcast_to(sums[at : at + 8, :], (8, 8)), 0.0)
        out[...] = jnp.sum(wide, axis=0, keepdims=True)


def zero_rows(acc, i):
    rows = pl.ds(pl.multiple_of(i * 64, 64), 64)
    for w in range(2):
        acc[w, rows, :] = jnp.zeros((64, acc.shape[2]), F32)


def body(hidden, lm_head, targets, segment, pad_mask, seq_bench):
    tok, width = hidden.shape
    voc = lm_head.shape[1]
    kp = width // PIECES
    tokens = GROUP * tok
    dma = pltpu.SemaphoreType.DMA
    anywhere = pl.BlockSpec(memory_space=pl.ANY)
    smem = pl.BlockSpec(memory_space=pltpu.SMEM)
    vmem = pl.BlockSpec(memory_space=pltpu.VMEM)
    nll, total, count = pl.pallas_call(
        kernel,
        out_shape=(
            jax.ShapeDtypeStruct((1, tok), F32),
            jax.ShapeDtypeStruct((1, NBENCH), F32),
            jax.ShapeDtypeStruct((1, NBENCH), F32),
        ),
        in_specs=[anywhere, anywhere, smem, smem, smem, smem],
        out_specs=(vmem, vmem, vmem),
        scratch_shapes=[
            pltpu.VMEM((PIECES, NA, tok, kp), jnp.bfloat16),
            pltpu.VMEM((NA * tok, kp), F32),
            pltpu.VMEM((PIECES, NB, NZ, NA * tok, kp), jnp.bfloat16),
            pltpu.VMEM((2, width, voc), jnp.bfloat16),
            pltpu.VMEM((2, tokens, voc), F32),
            pltpu.VMEM((tokens, 1), F32),
            pltpu.VMEM((NA + NB + NZ, 8, 128), F32),
            pltpu.VMEM((NA + NB + NZ, 8, 128), F32),
            pltpu.VMEM((2, 16, 128), F32),
            pltpu.VMEM((8, 128), F32),
            dma((PIECES,)), dma((PIECES,)), dma, dma((PIECES,)),
            dma, dma((PIECES, NA - 1)), dma, dma((PIECES, NZ - 1)),
            dma, dma((PIECES, 2, NZ)), dma, dma((PIECES, NZ)),
            dma((NA + NB + NZ,)), dma((NA + NB + NZ,)),
            dma((NA + NB + NZ,)), dma((NA + NB + NZ,)),
            dma, dma,
        ],
        compiler_params=pltpu.CompilerParams(
            collective_id=0, has_side_effects=True, vmem_limit_bytes=62 * 1024 * 1024
        ),
        name="nll",
    )(hidden, lm_head, targets, segment, pad_mask, seq_bench)
    return (nll.reshape(tok), total.reshape(NBENCH), count.reshape(NBENCH))


def solution(mesh):
    split = Mesh(mesh.devices.reshape(4, 2, 8, 4), AXES)
    return jax.shard_map(
        body,
        mesh=split,
        in_specs=(P(AXES, None), P(None, AXES), P(AXES), P(AXES), P(AXES), P()),
        out_specs=(P(AXES), P(), P()),
        check_vma=False,
    )
```

time: 265 us -> 96.3 us (0.36); the launches traced: 261 us -> 95.9 us
  blocking collectives: 141 us -> 0 us
  Pallas kernels: 0 us -> 80 us
  waiting for transfers between devices: 75.1 us -> 0 us
  matrix products: 14.3 us -> 0 us
  between operations: 14.9 us -> 0.64 us
  local copies, waits for them, and re-layouts: 2.32 us -> 15.3 us
  starting transfers between devices: 11.4 us -> 0 us
    all_gather x8 -> x0, blocking collectives: 92.5 us -> none  [the longest x4 42.9 us: gathered_once(): both, at, found = (lax.all_gather(jnp.concatenate(lines), axis), 0, {})]
    pallas_call x0 -> x1, Pallas kernels: none -> 80 us  [body(): pl.pallas_call(kernel, out_shape=(jax.ShapeDtypeStruct((1, tok), F32), ja...]
    all_gather x2 -> x0, waiting for transfers between devices: 75.1 us -> none  [the longest x1 41.4 us: whole_of(): out = lax.all_gather(out, axes[number], axis=dim, tiled=True)]
    psum x4 -> x0, blocking collectives: 41.7 us -> none  [one_axis_at_a_time(): return functools.reduce(lax.psum, axes, value)]
    dot_general x1 -> x0, matrix products: 14.3 us -> none  [shard_stats(): logits = jnp.dot(piece, lm_head, preferred_element_type=jnp.float32)]
    unnamed x15 -> x4, local copies, waits for them, and re-layouts: 1.69 us -> 15.3 us
    ppermute x1 -> x0, starting transfers between devices: 11.3 us -> none  [from_behind(): lax.ppermute(value, axis, [(source, source + steps) for source in range(l...]
    unnamed x1 -> x0, blocking collectives: 6.82 us -> none
  transfers between devices with their start and end apart: 3 -> 0, of which waited for: 2 -> 0; matrix products, arithmetic and copies ran while one was open for 7% -> 0% of each run, Pallas kernels for 0% -> 0%
where the time goes in v1:
time: 96.3 us; the launch traced here: 95.9 us
  Pallas kernels  80 us (83%)
  local copies, waits for them, and re-layouts  15.3 us (16%)
    pallas_call x1, Pallas kernels, body(): pl.pallas_call(kernel, out_shape=(jax.ShapeDtypeStruct((1, tok), F32), ja...  80 us
    unnamed x4, local copies, waits for them, and re-layouts  15.3 us

profile of v1, /device:TPU:1, one launch (start us, length us, event | category | flops | bytes accessed | tf_op | source)
XLA Modules:
  0.0 95.9 jit_solution(3880255881669039210)
XLA Ops:
  0.6 12.0 %copy.9.lm_head = bf16[8192,501]{1,0:T(8,128)(2,1)} copy(bf16[8192,501]{0,1:T(8,128)(2,1)} %param.7) | data formatting | bytes 16416768 | tf_op args[1]
  12.6 80.0 %nll.1 = (f32[1,4]{1,0:T(1,128)}, f32[1,8]{1,0:T(1,128)}, f32[1,8]{1,0:T(1,128)}) custom-call(bf16[4,8192]{1,0:T(4,128)(2,1)} %hidden.1, bf16[8192,501]{1,0:T(8,128)(2,1)} %copy.9.lm_head, s32[4]{0:T(128)} %targets.1, s32[4]{0:T(128)} %segment.1, s32[4]{0:T(128)} %pad_mask.1, s32[257]{0:T(512)} %seq_bench.1), custom_call_target="tpu_custom_call" | custom-call | tf_op jit(solution)/shard_map/nll/pallas_call | solution.py:343
  92.6 1.1 %copy.13 = f32[4]{0:T(128)} copy(f32[4]{0:T(128)} %bitcast.5) | data formatting | bytes 32
  93.7 1.1 %copy.14 = f32[8]{0:T(128)} copy(f32[8]{0:T(128)} %bitcast.4) | data formatting | bytes 64
  94.8 1.1 %copy.15 = f32[8]{0:T(128)} copy(f32[8]{0:T(128)} %bitcast.3) | data formatting | bytes 64

commit v2 on v1

--- a/solution.py
+++ b/solution.py
@@ -20,9 +20,9 @@
 
 
 def kernel(
-    hidden, lm_head, targets, segment, pad_mask, seq_bench,
-    nll_out, total_out, count_out,
-    abuf, rows32, gath, wbuf, acc, tcol, info, stat, last, nllbuf,
+    hidden, weights, targets, segment, pad_mask, seq_bench,
+    out,
+    abuf, rows32, gath, wbuf, acc, info, stat, last, nllbuf,
     lsem, wlsem, wsend, wrecv, asend, arecv, zsend, zrecv,
     bsend, brecv, fsend, frecv, isend, irecv, ssend, srecv, csend, crecv,
 ):
@@ -31,7 +31,7 @@
     a = y * (1 - c) + x * c
     b = x * (1 - c) + y * c
     kp = abuf.shape[3]
-    voc = lm_head.shape[1]
+    voc = weights.shape[0]
 
     def dev(a_, b_, z_, c_=None):
         if c_ is None:
@@ -60,12 +60,12 @@
         return pltpu.make_async_copy(hidden.at[:, cols], abuf.at[p, a], lsem.at[p])
 
     def own_weights(p):
-        rows = pl.ds(pl.multiple_of(p * kp, kp), kp)
-        return pltpu.make_async_copy(lm_head.at[rows, :], wbuf.at[0, rows, :], wlsem.at[p])
+        cols = pl.ds(pl.multiple_of(p * kp, kp), kp)
+        return pltpu.make_async_copy(weights.at[:, cols], wbuf.at[0, :, cols], wlsem.at[p])
 
     def swap_weights(p):
-        rows = pl.ds(pl.multiple_of(p * kp, kp), kp)
-        return rdma(lm_head.at[rows, :], wbuf.at[1, rows, :], wsend, wrecv.at[p], partner)
+        cols = pl.ds(pl.multiple_of(p * kp, kp), kp)
+        return rdma(weights.at[:, cols], wbuf.at[1, :, cols], wsend, wrecv.at[p], partner)
 
     def loop(n, body):
         lax.fori_loop(0, n, lambda i, _: (body(i), 0)[1], 0)
@@ -98,7 +98,7 @@
         own = jnp.where((row == b + 4) & (lane == base + t), code, own)
     own = own.astype(F32)
 
-    loop(acc.shape[1] // 64, lambda i: zero_rows(acc, i))
+    acc[...] = jnp.zeros(acc.shape, F32)
 
     pl.semaphore_wait(barrier, len(peers))
 
@@ -206,10 +206,12 @@
             f_copy(p, j).wait_recv()
         own_weights(p).wait()
         swap_weights(p).wait_recv()
-        rows = pl.ds(pl.multiple_of(p * kp, kp), kp)
+        cols = pl.ds(pl.multiple_of(p * kp, kp), kp)
+        rows = gath[p].reshape(acc.shape[2], kp)
         for w in range(2):
-            lhs = gath[p].reshape(acc.shape[1], kp)
-            acc[w] += jnp.dot(lhs, wbuf[w, rows, :], preferred_element_type=F32)
+            acc[w] += lax.dot_general(
+                wbuf[w, :, cols], rows, (((1,), (1,)), ((), ())), preferred_element_type=F32
+            )
 
     def at_piece(tick, lag, fn):
         p = tick - lag
@@ -217,10 +219,6 @@
         @pl.when((p >= 0) & (p < PIECES))
         def _():
             fn(p)
-
-    eye = lax.broadcasted_iota(jnp.int32, (128, 128), 0) == lax.broadcasted_iota(
-        jnp.int32, (128, 128), 1
-    )
 
     def ticks(tick):
         at_piece(tick, 0, step_0)
@@ -244,38 +242,27 @@
         @pl.when(tick == 6)
         def _():
             stage_wait(info, *sz, isend, irecv, to_z)
-            every = added(info, NA + NB, NZ)
-            info[0] = every
-            for k in range(4):
-                wide = jnp.where(eye, jnp.broadcast_to(every[k : k + 1, :], (128, 128)), 0.0)
-                tcol[k * 128 : (k + 1) * 128, :] = jnp.sum(wide, axis=1, keepdims=True)
+            info[0] = added(info, NA + NB, NZ)
 
     loop(PIECES + LAG, ticks)
 
     index = ((x * 2 + c) * NZ + z) * NB + y
     other = ((x * 2 + 1 - c) * NZ + z) * NB + y
-    lanes = lax.broadcasted_iota(jnp.int32, (128, voc), 1)
-    cols = [(lanes + i * voc).astype(F32) for i in (index, other)]
-
-    def statistics(k):
-        rows = pl.ds(pl.multiple_of(k * 128, 128), 128)
-        own_l, other_l = acc[0, rows, :], acc[1, rows, :]
-        wanted = tcol[rows, :]
-        top = jnp.maximum(
-            jnp.max(own_l, axis=1, keepdims=True), jnp.max(other_l, axis=1, keepdims=True)
+    entries = lax.broadcasted_iota(jnp.int32, (voc, 128), 0)
+    numbers = [(entries + i * voc).astype(F32) for i in (index, other)]
+    for k in range(4):
+        cols = slice(k * 128, (k + 1) * 128)
+        logits = [acc[w, :, cols] for w in range(2)]
+        wanted = info[0, k : k + 1, :]
+        tops = [jnp.max(part, axis=0, keepdims=True) for part in logits]
+        top = jnp.maximum(*tops)
+        total = sum(jnp.sum(jnp.exp(part - top), axis=0, keepdims=True) for part in logits)
+        picked = sum(
+            jnp.sum(jnp.where(number == wanted, part, 0.0), axis=0, keepdims=True)
+            for number, part in zip(numbers, logits)
         )
-        total = jnp.sum(jnp.exp(own_l - top), axis=1, keepdims=True) + jnp.sum(
-            jnp.exp(other_l - top), axis=1, keepdims=True
-        )
-        picked = jnp.sum(
-            jnp.where(cols[0] == wanted, own_l, 0.0), axis=1, keepdims=True
-        ) + jnp.sum(jnp.where(cols[1] == wanted, other_l, 0.0), axis=1, keepdims=True)
-        lse = top + jnp.log(total)
-        for at, value in ((0, lse), (4, picked)):
-            wide = jnp.where(eye, jnp.broadcast_to(value, (128, 128)), 0.0)
-            nllbuf[pl.ds(at + k, 1), :] = jnp.sum(wide, axis=0, keepdims=True)
-
-    loop(4, statistics)
+        nllbuf[k : k + 1, :] = top + jnp.log(total)
+        nllbuf[k + 4 : k + 5, :] = picked
 
     def merged(buf, at, n):
         parts = [buf[at + k] for k in range(n)]
@@ -309,26 +296,19 @@
     nllbuf[0:4, :] = nll
     mine = nllbuf[pl.ds(b, 1), :]
     rolled = pltpu.roll(jnp.broadcast_to(mine, (8, 128)), lax.rem(128 - base, 128), 1)
-    nll_out[...] = rolled[0:1, 0:4]
 
     rdma(abuf.at[:, 0:3], abuf.at[:, 0:3], asend, arecv.at[0, 0], partner).wait_send()
-    rdma(wbuf.at[1], wbuf.at[1], wsend, wrecv.at[0], partner).wait_send()
+    rdma(weights, wbuf.at[1], wsend, wrecv.at[0], partner).wait_send()
     rdma(gath.at[:, 0, 0:7], gath.at[:, 0, 0:7], zsend, zrecv.at[0, 0], partner).wait_send()
     rdma(gath.at[:, 0:2], gath.at[:, 0:2], bsend, brecv.at[0, 0, 0], partner).wait_send()
     rdma(gath.at[:, 0], gath.at[:, 0], fsend, frecv.at[0, 0], partner).wait_send()
 
     swap.wait()
     sums = jnp.sum(last[0] + last[1], axis=1, keepdims=True)
-    small = lax.broadcasted_iota(jnp.int32, (8, 8), 0) == lax.broadcasted_iota(jnp.int32, (8, 8), 1)
-    for out, at in ((total_out, 0), (count_out, 8)):
-        wide = jnp.where(small, jnp.broadcast_to(sums[at : at + 8, :], (8, 8)), 0.0)
-        out[...] = jnp.sum(wide, axis=0, keepdims=True)
-
-
-def zero_rows(acc, i):
-    rows = pl.ds(pl.multiple_of(i * 64, 64), 64)
-    for w in range(2):
-        acc[w, rows, :] = jnp.zeros((64, acc.shape[2]), F32)
+    row16 = lax.broadcasted_iota(jnp.int32, (16, 128), 0)
+    lane16 = lax.broadcasted_iota(jnp.int32, (16, 128), 1)
+    sums = jnp.sum(jnp.where(lane16 == row16 + 4, sums, 0.0), axis=0, keepdims=True)
+    out[...] = jnp.where(lane[0:1, :] < 4, rolled[0:1, :], sums)
 
 
 def body(hidden, lm_head, targets, segment, pad_mask, seq_bench):
@@ -340,22 +320,17 @@
     anywhere = pl.BlockSpec(memory_space=pl.ANY)
     smem = pl.BlockSpec(memory_space=pltpu.SMEM)
     vmem = pl.BlockSpec(memory_space=pltpu.VMEM)
-    nll, total, count = pl.pallas_call(
+    out = pl.pallas_call(
         kernel,
-        out_shape=(
-            jax.ShapeDtypeStruct((1, tok), F32),
-            jax.ShapeDtypeStruct((1, NBENCH), F32),
-            jax.ShapeDtypeStruct((1, NBENCH), F32),
-        ),
+        out_shape=jax.ShapeDtypeStruct((1, 128), F32),
         in_specs=[anywhere, anywhere, smem, smem, smem, smem],
-        out_specs=(vmem, vmem, vmem),
+        out_specs=vmem,
         scratch_shapes=[
             pltpu.VMEM((PIECES, NA, tok, kp), jnp.bfloat16),
             pltpu.VMEM((NA * tok, kp), F32),
             pltpu.VMEM((PIECES, NB, NZ, NA * tok, kp), jnp.bfloat16),
-            pltpu.VMEM((2, width, voc), jnp.bfloat16),
-            pltpu.VMEM((2, tokens, voc), F32),
-            pltpu.VMEM((tokens, 1), F32),
+            pltpu.VMEM((2, voc, width), jnp.bfloat16),
+            pltpu.VMEM((2, voc, tokens), F32),
             pltpu.VMEM((NA + NB + NZ, 8, 128), F32),
             pltpu.VMEM((NA + NB + NZ, 8, 128), F32),
             pltpu.VMEM((2, 16, 128), F32),
@@ -371,8 +346,9 @@
             collective_id=0, has_side_effects=True, vmem_limit_bytes=62 * 1024 * 1024
         ),
         name="nll",
-    )(hidden, lm_head, targets, segment, pad_mask, seq_bench)
-    return (nll.reshape(tok), total.reshape(NBENCH), count.reshape(NBENCH))
+    )(hidden, lm_head.T, targets, segment, pad_mask, seq_bench)
+    line = out[0]
+    return (line[:tok], line[tok : tok + NBENCH], line[tok + NBENCH : tok + 2 * NBENCH])
 
 
 def solution(mesh):

time: 96.3 us -> 82.7 us (0.86)
  local copies, waits for them, and re-layouts: 15.3 us -> 2.37 us
    unnamed x4 -> x0, local copies, waits for them, and re-layouts: 15.3 us -> none
    slice x0 -> x2, local copies, waits for them, and re-layouts: none -> 2.37 us  [the longest x1 1.26 us: body(): line[tok + NBENCH:tok + 2 * NBENCH]]
where the time goes in v2:
time: 82.7 us; the launch traced here: 82.6 us
  Pallas kernels  79.6 us (96%)
  local copies, waits for them, and re-layouts  2.37 us (3%)
    pallas_call x1, Pallas kernels, body(): pl.pallas_call(kernel, out_shape=jax.ShapeDtypeStruct((1, 128), F32), in_...  79.6 us

profile of v2, /device:TPU:1, one launch (start us, length us, event | category | flops | bytes accessed | tf_op | source)
XLA Modules:
  0.0 82.6 jit_solution(6498887225623827301)
XLA Ops:
  0.6 79.6 %nll.1 = f32[1,128]{1,0:T(1,128)} custom-call(bf16[4,8192]{1,0:T(4,128)(2,1)} %hidden.1, bf16[501,8192]{1,0:T(8,128)(2,1)} %bitcast.7, s32[4]{0:T(128)} %targets.1, s32[4]{0:T(128)} %segment.1, s32[4]{0:T(128)} %pad_mask.1, s32[257]{0:T(512)} %seq_bench.1), custom_call_target="tpu_custom_call" | custom-call | tf_op jit(solution)/shard_map/nll/pallas_call | solution.py:323
  80.2 1.3 %slice_bitcast_fusion = (f32[8]{0:T(128)}, f32[8]{0:T(128)}) fusion(f32[1,128]{1,0:T(1,128)} %nll.1), kind=kLoop, calls=%fused_computation | loop fusion | bytes 128 | tf_op jit(solution)/shard_map/slice | solution.py:351
  81.5 1.1 %slice_bitcast_fusion.2 = f32[4]{0:T(128)} fusion(f32[1,128]{1,0:T(1,128)} %nll.1), kind=kLoop, calls=%fused_computation.2 | loop fusion | bytes 32 | tf_op jit(solution)/shard_map/slice | solution.py:351

commit v3 on v2

v3 whole, which is shorter than its diff:
```python
import functools

import jax
import jax.numpy as jnp
from jax import lax
from jax.experimental import pallas as pl
from jax.experimental.pallas import tpu as pltpu
from jax.sharding import Mesh
from jax.sharding import PartitionSpec as P

NBENCH = 8
AXES = ("dp_0", "dp_1", "vocab_0", "vocab_1")
NA, NB, NZ = 4, 4, 8
PIECES = 8
LAST = PIECES - 1
LAG = 6
GROUP = NA * NB * NZ
DIST = (0, NZ - 1, 1, NZ - 2, 2, NZ - 3, 3, 4)
MESH = pl.DeviceIdType.MESH
F32 = jnp.float32


def kernel(
    hidden, weights, targets, segment, pad_mask, seq_bench,
    out,
    tgt_s, seg_s, pad_s, ben_s,
    abuf, rows32, gath, wbuf, acc, info, stat, last, nllbuf,
    small, lsem, wlsem, wsend, wrecv, asend, arecv, zsend, zrecv,
    bsend, brecv, fsend, frecv, ebsend, ebrecv, ezsend, ezrecv,
    isend, irecv, ssend, srecv, csend, crecv,
):
    x, c = lax.axis_index("dp_0"), lax.axis_index("dp_1")
    z, y = lax.axis_index("vocab_0"), lax.axis_index("vocab_1")
    a = y * (1 - c) + x * c
    b = x * (1 - c) + y * c
    kp = abuf.shape[3]
    voc = weights.shape[0]

    def dev(a_, b_, z_):
        return (b_ * (1 - c) + a_ * c, c, z_, a_ * (1 - c) + b_ * c)

    def rdma(src, dst, ssem, rsem, to):
        return pltpu.make_async_remote_copy(
            src_ref=src, dst_ref=dst, send_sem=ssem, recv_sem=rsem,
            device_id=to, device_id_type=MESH,
        )

    def a_at(k):
        return lax.rem(a + k, NA)

    def b_at(k):
        return lax.rem(b + k, NB)

    def z_at(k):
        return lax.rem(z + k, NZ)

    partner = (x, 1 - c, z, y)

    def columns(p):
        return pl.ds(pl.multiple_of(p * kp, kp), kp)

    def own_hidden(p):
        return pltpu.make_async_copy(hidden.at[:, columns(p)], abuf.at[p, a], lsem.at[p])

    def own_weights(p):
        cols = columns(p)
        return pltpu.make_async_copy(weights.at[:, cols], wbuf.at[0, :, cols], wlsem.at[p])

    def swap_weights(p):
        cols = columns(p)
        return rdma(weights.at[:, cols], wbuf.at[1, :, cols], wsend, wrecv.at[p], partner)

    def loop(n, fn):
        lax.fori_loop(0, n, lambda i, _: (fn(i), 0)[1], 0)

    def turn(i):
        return lax.rem(i + LAST, PIECES)

    loop(PIECES, lambda i: own_hidden(turn(i)).start())
    smalls = [
        pltpu.make_async_copy(src, dst, small.at[k])
        for k, (src, dst) in enumerate(
            ((targets, tgt_s), (segment, seg_s), (pad_mask, pad_s), (seq_bench, ben_s))
        )
    ]
    for copy in smalls:
        copy.start()

    barrier = pltpu.get_barrier_semaphore()
    peers = [dev(a_at(k), b, z) for k in range(1, NA)]
    peers += [dev(a, b_at(k), z) for k in (1, NB - 1)]
    peers += [dev(a, b, z_at(k)) for k in (1, NZ - 1)]
    peers += [partner]
    for peer in peers:
        pl.semaphore_signal(barrier, inc=1, device_id=peer, device_id_type=MESH)
    pl.semaphore_wait(barrier, len(peers))

    def a_copy(p, k):
        return rdma(abuf.at[p, a], abuf.at[p, a], asend, arecv.at[p, k - 1], dev(a_at(k), b, z))

    def a_start(i):
        p = turn(i)
        own_hidden(p).wait()
        for k in range(1, NA):
            a_copy(p, k).start()

    loop(PIECES, a_start)
    loop(PIECES, lambda p: own_weights(p).start())
    loop(PIECES, lambda p: swap_weights(p).start())
    acc[...] = jnp.zeros(acc.shape, F32)

    def planes(buf, ssem, rsem):
        at = a * NB + b
        return [
            rdma(buf.at[at], buf.at[at], ssem.at[k], rsem.at[k], dev(a_at(k // NB), b_at(k % NB), z))
            for k in range(1, NA * NB)
        ]

    def lines(buf, ssem, rsem):
        at = NA * NB + z
        return [
            rdma(
                buf.at[at], buf.at[at], ssem.at[NA * NB + k], rsem.at[NA * NB + k],
                dev(a, b, z_at(k)),
            )
            for k in range(1, NZ)
        ]

    def start_all(copies):
        for copy in copies:
            copy.start()

    def wait_all(copies):
        for copy in copies:
            copy.wait()

    def added(buf, at, n):
        total = buf[at]
        for k in range(1, n):
            total = total + buf[at + k]
        return total

    def block(p, b_, z_):
        return gath.at[p, z_, b_]

    def z_copy(p, b_, k, ssem, rsem, up):
        zi = z_at(k)
        return rdma(block(p, b_, zi), block(p, b_, zi), ssem, rsem, dev(a, b, z_at(up)))

    def b_send(p, zi, b_, ssem, rsem, go):
        return rdma(block(p, b_, zi), block(p, b_, zi), ssem, rsem, dev(a, b_at(go), z))

    def b_copy(p, j, way):
        go = 1 if way == 0 else NB - 1
        return b_send(p, z_at(DIST[j]), b, bsend, brecv.at[p, way, j], go)

    def f_copy(p, j):
        come, go = (NB - 1, 1) if j % 2 == 0 else (1, NB - 1)
        return b_send(p, z_at(DIST[j]), b_at(come), fsend, frecv.at[p, j], go)

    def b_both(p, j):
        b_copy(p, j, 0).start()
        b_copy(p, j, 1).start()

    def tile_rows(p):
        for k in range(1, NA):
            a_copy(p, k).wait_recv()
        for k in range(NA):
            rows32[4 * k : 4 * k + 4, :] = abuf[p, k].astype(F32)
        gath[p, z, b] = rows32[...].astype(jnp.bfloat16)

    def e_copy(k, src, go):
        return b_send(LAST, z, b_at(src), ebsend, ebrecv.at[k], go)

    tile_rows(LAST)
    e_copy(0, 0, 1).start()
    e_copy(1, 0, NB - 1).start()

    def begin(p):
        tile_rows(p)
        b_both(p, 0)

        @pl.when(p == 0)
        def _():
            z_step(p, 0, p, b, zsend, zrecv)

    def z_step(p, s, u, b_, ssem, rsem):
        if s == 0:
            z_copy(p, b_, 0, ssem, rsem.at[u, 0], 1).start()
            z_copy(p, b_, 0, ssem, rsem.at[u, 1], NZ - 1).start()
        elif s < 4:
            odd = lax.rem(u, 2)
            z_copy(p, b_, NZ - s, ssem, rsem.at[u, 2 * s - 2], 1).wait_recv()
            if s < 3:
                z_copy(p, b_, NZ - s, ssem, rsem.at[u, 2 * s], 1).start()
            z_copy(p, b_, s, ssem, rsem.at[u, 2 * s - 1], NZ - 1).wait_recv()
            if s < 3:
                z_copy(p, b_, s, ssem, rsem.at[u, 2 * s + 1], NZ - 1).start()
            else:
                z_copy(p, b_, 5 + 6 * odd, ssem, rsem.at[u, 6], 1 + 6 * odd).start()
        else:
            z_copy(p, b_, 4, ssem, rsem.at[u, 6], 1).wait_recv()

    loop(LAST, begin)

    def step(p, s):
        z_step(p, s, p, b, zsend, zrecv)
        if 0 < s < 4:
            b_both(p, 2 * s - 1)
            b_both(p, 2 * s)
        elif s == 4:
            b_both(p, 7)

    def e_step(u, s):
        b_ = b_at(u + (u // 2) * (5 - 2 * u))
        z_step(LAST, s, u, b_, ezsend, ezrecv)

    def forward(p, s):
        for j in ((0,), (1, 2), (3, 4), (5, 6), (7,))[s]:
            b_copy(p, j, j % 2).wait_recv()
            f_copy(p, j).start()

    def product(p):
        own_weights(p).wait()
        swap_weights(p).wait_recv()
        cols = columns(p)
        rows = gath[p].reshape(acc.shape[2], kp)
        for w in range(2):
            acc[w] += lax.dot_general(
                wbuf[w, :, cols], rows, (((1,), (1,)), ((), ())), preferred_element_type=F32
            )

    def multiply(p):
        @pl.when(p < LAST)
        def _():
            for j in range(8):
                b_copy(p, j, 1 - j % 2).wait_recv()
                f_copy(p, j).wait_recv()

        product(p)

    def at_piece(tick, lag, fn):
        p = tick - lag

        @pl.when((p >= 0) & (p < LAST))
        def _():
            fn(p)

    row = lax.broadcasted_iota(jnp.int32, (8, 128), 0)
    lane = lax.broadcasted_iota(jnp.int32, (8, 128), 1)
    base = b * 16 + a * 4

    def own_info():
        own = jnp.zeros((8, 128), jnp.int32)
        whole_last = (x == NA - 1) & (c == 1) & (z == NZ - 1) & (y == NB - 1)
        for t in range(4):
            seg = seg_s[t]
            if t < 3:
                kept = (pad_s[t] == 1) & (seg == seg_s[t + 1])
            else:
                kept = (pad_s[t] == 1) & jnp.logical_not(whole_last)
            code = jnp.where(kept, ben_s[seg], NBENCH)
            own = jnp.where((row == z) & (lane == base + t), tgt_s[t], own)
            own = jnp.where((row == z) & (lane == base + t + 64), code, own)
        return own.astype(F32)

    def ticks(tick):
        @pl.when(tick > 0)
        def _():
            at_piece(tick, 0, functools.partial(step, s=0))

        for s in range(1, 5):
            at_piece(tick, s, functools.partial(step, s=s))

        @pl.when(tick == 1)
        def _():
            e_copy(0, 0, 1).wait_recv()
            e_copy(1, 0, NB - 1).wait_recv()
            e_copy(2, NB - 1, 1).start()

        @pl.when(tick == 3)
        def _():
            e_copy(2, NB - 1, 1).wait_recv()

        for s in range(5):
            at_piece(tick, s + 1, functools.partial(forward, s=s))

        for s in range(5):
            twice = tick - 1 - s

            @pl.when((twice >= 0) & (twice < 2 * NB) & (lax.rem(twice, 2) == 0))
            def _():
                e_step(twice // 2, s)

        @pl.when((tick >= LAG) & (tick < LAG + LAST - 1))
        def _():
            multiply(tick - LAG)

        @pl.when(tick == 7)
        def _():
            wait_all(smalls)
            info[a * NB + b] = own_info()
            start_all(planes(info, isend, irecv))

        @pl.when(tick == 9)
        def _():
            wait_all(planes(info, isend, irecv))
            info[NA * NB + z] = added(info, 0, NA * NB)
            start_all(lines(info, isend, irecv))

        @pl.when(tick == 11)
        def _():
            wait_all(lines(info, isend, irecv))
            info[0] = added(info, NA * NB, NZ)

    loop(LAG + LAST - 1, ticks)
    loop(2, lambda i: multiply(LAST - i))

    index = ((x * 2 + c) * NZ + z) * NB + y
    other = ((x * 2 + 1 - c) * NZ + z) * NB + y
    entries = lax.broadcasted_iota(jnp.int32, (voc, 128), 0)
    numbers = [(entries + i * voc).astype(F32) for i in (index, other)]
    left = lane[0:1, :] < 64
    every = info[0]

    def over(line):
        return pltpu.roll(jnp.broadcast_to(line, (8, 128)), 64, 1)[0:1, :]

    for k in range(4):
        cols = slice(k * 128, (k + 1) * 128)
        logits = [acc[w, :, cols] for w in range(2)]
        wanted = jnp.where(left, every[2 * k : 2 * k + 1, :], over(every[2 * k + 1 : 2 * k + 2, :]))
        tops = [jnp.max(part, axis=0, keepdims=True) for part in logits]
        top = jnp.maximum(*tops)
        total = sum(jnp.sum(jnp.exp(part - top), axis=0, keepdims=True) for part in logits)
        picked = sum(
            jnp.sum(jnp.where(number == wanted, part, 0.0), axis=0, keepdims=True)
            for number, part in zip(numbers, logits)
        )
        lse = top + jnp.log(total)
        nllbuf[2 * k : 2 * k + 1, :] = jnp.where(left, lse, over(picked))
        nllbuf[2 * k + 1 : 2 * k + 2, :] = jnp.where(left, over(lse), picked)

    def merged(buf, at, n):
        parts = [buf[at + k] for k in range(n)]
        top = functools.reduce(jnp.maximum, parts)
        total = functools.reduce(jnp.add, [jnp.exp(part - top) for part in parts])
        picked = functools.reduce(jnp.add, parts)
        return jnp.where(lane < 64, top + jnp.log(total), picked)

    stat[a * NB + b] = nllbuf[...]
    start_all(planes(stat, ssend, srecv))
    wait_all(planes(stat, ssend, srecv))
    stat[NA * NB + z] = merged(stat, 0, NA * NB)
    start_all(lines(stat, ssend, srecv))
    wait_all(lines(stat, ssend, srecv))
    both = merged(stat, NA * NB, NZ)
    nll = both - pltpu.roll(both, 64, 1)

    codes = jnp.where(lane < 64, pltpu.roll(every, 64, 1), float(NBENCH))
    last_t, last_c = jnp.zeros((8, 128), F32), jnp.zeros((8, 128), F32)
    for j in range(NBENCH):
        hit = codes == float(j)
        part_t = jnp.sum(jnp.where(hit, nll, 0.0), axis=0, keepdims=True)
        part_c = jnp.sum(jnp.where(hit, 1.0, 0.0), axis=0, keepdims=True)
        last_t = jnp.where(row == j, part_t, last_t)
        last_c = jnp.where(row == j, part_c, last_c)
    last[c, 0:8, :] = last_t
    last[c, 8:16, :] = last_c
    swap = rdma(last.at[c], last.at[c], csend, crecv, partner)
    swap.start()

    nllbuf[...] = nll
    mine = nllbuf[pl.ds(z, 1), :]
    rolled = pltpu.roll(jnp.broadcast_to(mine, (8, 128)), lax.rem(128 - base, 128), 1)

    def left_all(ref, ssem, rsem):
        rdma(ref, ref, ssem, rsem, partner).wait_send()

    left_all(abuf.at[:, 0:3], asend, arecv.at[0, 0])
    rdma(weights, wbuf.at[1], wsend, wrecv.at[0], partner).wait_send()
    left_all(gath.at[0:LAST, 0:7, 0], zsend, zrecv.at[0, 0])
    left_all(gath.at[0:LAST, 0:4], bsend, brecv.at[0, 0, 0])
    left_all(gath.at[0:LAST, 0:2], fsend, frecv.at[0, 0])
    left_all(gath.at[LAST, 0, 0:3], ebsend, ebrecv.at[0])
    left_all(gath.at[LAST, 0:7], ezsend, ezrecv.at[0, 0])

    swap.wait()
    sums = jnp.sum(last[0] + last[1], axis=1, keepdims=True)
    row16 = lax.broadcasted_iota(jnp.int32, (16, 128), 0)
    lane16 = lax.broadcasted_iota(jnp.int32, (16, 128), 1)
    sums = jnp.sum(jnp.where(lane16 == row16 + 4, sums, 0.0), axis=0, keepdims=True)
    out[...] = jnp.where(lane[0:1, :] < 4, rolled[0:1, :], sums)


def body(hidden, lm_head, targets, segment, pad_mask, seq_bench):
    tok, width = hidden.shape
    voc = lm_head.shape[1]
    kp = width // PIECES
    tokens = GROUP * tok
    dma = pltpu.SemaphoreType.DMA
    anywhere = pl.BlockSpec(memory_space=pl.ANY)
    vmem = pl.BlockSpec(memory_space=pltpu.VMEM)
    out = pl.pallas_call(
        kernel,
        out_shape=jax.ShapeDtypeStruct((1, 128), F32),
        in_specs=[anywhere] * 6,
        out_specs=vmem,
        scratch_shapes=[
            pltpu.SMEM((tok,), jnp.int32),
            pltpu.SMEM((tok,), jnp.int32),
            pltpu.SMEM((tok,), jnp.int32),
            pltpu.SMEM(seq_bench.shape, jnp.int32),
            pltpu.VMEM((PIECES, NA, tok, kp), jnp.bfloat16),
            pltpu.VMEM((NA * tok, kp), F32),
            pltpu.VMEM((PIECES, NZ, NB, NA * tok, kp), jnp.bfloat16),
            pltpu.VMEM((2, voc, width), jnp.bfloat16),
            pltpu.VMEM((2, voc, tokens), F32),
            pltpu.VMEM((NA * NB + NZ, 8, 128), F32),
            pltpu.VMEM((NA * NB + NZ, 8, 128), F32),
            pltpu.VMEM((2, 16, 128), F32),
            pltpu.VMEM((8, 128), F32),
            dma((4,)), dma((PIECES,)), dma((PIECES,)), dma, dma((PIECES,)),
            dma, dma((PIECES, NA - 1)), dma, dma((LAST, NZ - 1)),
            dma, dma((LAST, 2, NZ)), dma, dma((LAST, NZ)),
            dma, dma((3,)), dma, dma((NB, NZ - 1)),
            dma((NA * NB + NZ,)), dma((NA * NB + NZ,)),
            dma((NA * NB + NZ,)), dma((NA * NB + NZ,)),
            dma, dma,
        ],
        compiler_params=pltpu.CompilerParams(
            collective_id=0, has_side_effects=True, vmem_limit_bytes=62 * 1024 * 1024
        ),
        name="nll",
    )(hidden, lm_head.T, targets, segment, pad_mask, seq_bench)
    line = out[0]
    return (line[:tok], line[tok : tok + NBENCH], line[tok + NBENCH : tok + 2 * NBENCH])


def solution(mesh):
    split = Mesh(mesh.devices.reshape(4, 2, 8, 4), AXES)
    return jax.shard_map(
        body,
        mesh=split,
        in_specs=(P(AXES, None), P(None, AXES), P(AXES), P(AXES), P(AXES), P()),
        out_specs=(P(AXES), P(), P()),
        check_vma=False,
    )
```

time: 82.7 us -> 76.8 us (0.929)
  Pallas kernels: 79.6 us -> 73.7 us
    pallas_call x1, Pallas kernels: 79.6 us -> 73.7 us  [body(): pl.pallas_call(kernel, out_shape=jax.ShapeDtypeStruct((1, 128), F32), in_...]
where the time goes in v3:
time: 76.8 us; the launch traced here: 76.7 us
  Pallas kernels  73.7 us (96%)
  local copies, waits for them, and re-layouts  2.37 us (3%)
    pallas_call x1, Pallas kernels, body(): pl.pallas_call(kernel, out_shape=jax.ShapeDtypeStruct((1, 128), F32), in_...  73.7 us

profile of v3, /device:TPU:1, one launch (start us, length us, event | category | flops | bytes accessed | tf_op | source)
XLA Modules:
  0.0 76.7 jit_solution(4678714359436409885)
XLA Ops:
  0.6 73.7 %nll.1 = f32[1,128]{1,0:T(1,128)} custom-call(bf16[4,8192]{1,0:T(4,128)(2,1)} %hidden.1, bf16[501,8192]{1,0:T(8,128)(2,1)} %bitcast.7, s32[4]{0:T(128)} %targets.1, s32[4]{0:T(128)} %segment.1, s32[4]{0:T(128)} %pad_mask.1, s32[257]{0:T(512)} %seq_bench.1), custom_call_target="tpu_custom_call" | custom-call | tf_op jit(solution)/shard_map/nll/pallas_call | solution.py:404
  74.4 1.3 %slice_bitcast_fusion = (f32[8]{0:T(128)}, f32[8]{0:T(128)}) fusion(f32[1,128]{1,0:T(1,128)} %nll.1), kind=kLoop, calls=%fused_computation | loop fusion | bytes 128 | tf_op jit(solution)/shard_map/slice | solution.py:437
  75.6 1.1 %slice_bitcast_fusion.2 = f32[4]{0:T(128)} fusion(f32[1,128]{1,0:T(1,128)} %nll.1), kind=kLoop, calls=%fused_computation.2 | loop fusion | bytes 32 | tf_op jit(solution)/shard_map/slice | solution.py:437

commit v4 on v3

--- a/solution.py
+++ b/solution.py
@@ -13,9 +13,13 @@
 NA, NB, NZ = 4, 4, 8
 PIECES = 8
 LAST = PIECES - 1
-LAG = 6
 GROUP = NA * NB * NZ
-DIST = (0, NZ - 1, 1, NZ - 2, 2, NZ - 3, 3, 4)
+PLAN = {
+    (1, 3): [(0, 0)], (1, 5): [(1, 0)], (1, 6): [(2, 0)], (2, 0): [(3, 0)], (2, 3): [(0, 1)],
+    (3, 0): [(1, 1)], (3, 1): [(2, 1)], (3, 4): [(3, 1)],
+    (4, 1): [(0, 2), (1, 2)], (4, 2): [(2, 2)], (4, 3): [(3, 2)], (4, 5): [(0, 3)],
+    (4, 6): [(1, 3)], (4, 7): [(2, 3), (3, 3)], (4, 8): [(0, 4), (1, 4), (2, 4), (3, 4)],
+}
 MESH = pl.DeviceIdType.MESH
 F32 = jnp.float32
 
@@ -140,6 +144,10 @@
             total = total + buf[at + k]
         return total
 
+    def dist(j, odd=None):
+        odd = j % 2 if odd is None else odd
+        return NZ - 1 - j // 2 if odd else j // 2
+
     def block(p, b_, z_):
         return gath.at[p, z_, b_]
 
@@ -150,13 +158,14 @@
     def b_send(p, zi, b_, ssem, rsem, go):
         return rdma(block(p, b_, zi), block(p, b_, zi), ssem, rsem, dev(a, b_at(go), z))
 
-    def b_copy(p, j, way):
+    def b_copy(p, j, way, odd=None):
         go = 1 if way == 0 else NB - 1
-        return b_send(p, z_at(DIST[j]), b, bsend, brecv.at[p, way, j], go)
-
-    def f_copy(p, j):
-        come, go = (NB - 1, 1) if j % 2 == 0 else (1, NB - 1)
-        return b_send(p, z_at(DIST[j]), b_at(come), fsend, frecv.at[p, j], go)
+        return b_send(p, z_at(dist(j, odd)), b, bsend, brecv.at[p, way, j], go)
+
+    def f_copy(p, j, odd=None):
+        odd = j % 2 if odd is None else odd
+        come, go = (1, NB - 1) if odd else (NB - 1, 1)
+        return b_send(p, z_at(dist(j, odd)), b_at(come), fsend, frecv.at[p, j], go)
 
     def b_both(p, j):
         b_copy(p, j, 0).start()
@@ -180,9 +189,7 @@
         tile_rows(p)
         b_both(p, 0)
 
-        @pl.when(p == 0)
-        def _():
-            z_step(p, 0, p, b, zsend, zrecv)
+        z_step(p, 0, p, b, zsend, zrecv)
 
     def z_step(p, s, u, b_, ssem, rsem):
         if s == 0:
@@ -220,31 +227,26 @@
             b_copy(p, j, j % 2).wait_recv()
             f_copy(p, j).start()
 
-    def product(p):
-        own_weights(p).wait()
-        swap_weights(p).wait_recv()
+    def multiply(p, h):
+        @pl.when(p < LAST)
+        def _():
+            for k in range(4):
+                b_copy(p, 4 * h + k, 1 - k % 2, k % 2).wait_recv()
+                f_copy(p, 4 * h + k, k % 2).wait_recv()
+
+        @pl.when(h == 0)
+        def _():
+            own_weights(p).wait()
+            swap_weights(p).wait_recv()
+
         cols = columns(p)
-        rows = gath[p].reshape(acc.shape[2], kp)
+        rows = jnp.concatenate(
+            [gath[p, z_at(dist(4 * h + k, k % 2))].reshape(NB * 16, kp) for k in range(4)], axis=0
+        )
         for w in range(2):
-            acc[w] += lax.dot_general(
+            acc[h, w] += lax.dot_general(
                 wbuf[w, :, cols], rows, (((1,), (1,)), ((), ())), preferred_element_type=F32
             )
-
-    def multiply(p):
-        @pl.when(p < LAST)
-        def _():
-            for j in range(8):
-                b_copy(p, j, 1 - j % 2).wait_recv()
-                f_copy(p, j).wait_recv()
-
-        product(p)
-
-    def at_piece(tick, lag, fn):
-        p = tick - lag
-
-        @pl.when((p >= 0) & (p < LAST))
-        def _():
-            fn(p)
 
     row = lax.broadcasted_iota(jnp.int32, (8, 128), 0)
     lane = lax.broadcasted_iota(jnp.int32, (8, 128), 1)
@@ -264,57 +266,62 @@
             own = jnp.where((row == z) & (lane == base + t + 64), code, own)
         return own.astype(F32)
 
-    def ticks(tick):
-        @pl.when(tick > 0)
+    def planned(s, i, count):
+        for at in range(count):
+            if (s, at) in PLAN:
+
+                @pl.when(i == at)
+                def _():
+                    for u, k in PLAN[s, at]:
+                        e_step(u, k)
+
+    def level(s, p):
+        if s == 1:
+
+            @pl.when(p == 0)
+            def _():
+                e_copy(0, 0, 1).wait_recv()
+                e_copy(1, 0, NB - 1).wait_recv()
+                e_copy(2, NB - 1, 1).start()
+
+            @pl.when(p == 6)
+            def _():
+                e_copy(2, NB - 1, 1).wait_recv()
+
+        planned(s, p, LAST)
+        step(p, s)
+        forward(p, s - 1)
+
+    for s in range(1, 4):
+        loop(LAST, functools.partial(level, s))
+
+    def finish(i):
+        planned(4, i, PIECES + 1)
+
+        @pl.when(i < LAST)
         def _():
-            at_piece(tick, 0, functools.partial(step, s=0))
-
-        for s in range(1, 5):
-            at_piece(tick, s, functools.partial(step, s=s))
-
-        @pl.when(tick == 1)
-        def _():
-            e_copy(0, 0, 1).wait_recv()
-            e_copy(1, 0, NB - 1).wait_recv()
-            e_copy(2, NB - 1, 1).start()
-
-        @pl.when(tick == 3)
-        def _():
-            e_copy(2, NB - 1, 1).wait_recv()
-
-        for s in range(5):
-            at_piece(tick, s + 1, functools.partial(forward, s=s))
-
-        for s in range(5):
-            twice = tick - 1 - s
-
-            @pl.when((twice >= 0) & (twice < 2 * NB) & (lax.rem(twice, 2) == 0))
-            def _():
-                e_step(twice // 2, s)
-
-        @pl.when((tick >= LAG) & (tick < LAG + LAST - 1))
-        def _():
-            multiply(tick - LAG)
-
-        @pl.when(tick == 7)
+            step(i, 4)
+            forward(i, 3)
+
+        @pl.when(i == 1)
         def _():
             wait_all(smalls)
             info[a * NB + b] = own_info()
             start_all(planes(info, isend, irecv))
 
-        @pl.when(tick == 9)
+        @pl.when(i == LAST)
         def _():
+            loop(LAST, lambda p: forward(p, 4))
             wait_all(planes(info, isend, irecv))
             info[NA * NB + z] = added(info, 0, NA * NB)
             start_all(lines(info, isend, irecv))
 
-        @pl.when(tick == 11)
-        def _():
-            wait_all(lines(info, isend, irecv))
-            info[0] = added(info, NA * NB, NZ)
-
-    loop(LAG + LAST - 1, ticks)
-    loop(2, lambda i: multiply(LAST - i))
+        h = i // PIECES
+        multiply(lax.rem(i + h * LAST, PIECES), h)
+
+    loop(2 * PIECES, finish)
+    wait_all(lines(info, isend, irecv))
+    info[0] = added(info, NA * NB, NZ)
 
     index = ((x * 2 + c) * NZ + z) * NB + y
     other = ((x * 2 + 1 - c) * NZ + z) * NB + y
@@ -327,9 +334,9 @@
         return pltpu.roll(jnp.broadcast_to(line, (8, 128)), 64, 1)[0:1, :]
 
     for k in range(4):
-        cols = slice(k * 128, (k + 1) * 128)
-        logits = [acc[w, :, cols] for w in range(2)]
-        wanted = jnp.where(left, every[2 * k : 2 * k + 1, :], over(every[2 * k + 1 : 2 * k + 2, :]))
+        ends = [pl.ds(z_at(dist(2 * k + m)), 1) for m in range(2)]
+        logits = [acc[k // 2, w, :, (k % 2) * 128 : (k % 2 + 1) * 128] for w in range(2)]
+        wanted = jnp.where(left, info[0, ends[0], :], over(info[0, ends[1], :]))
         tops = [jnp.max(part, axis=0, keepdims=True) for part in logits]
         top = jnp.maximum(*tops)
         total = sum(jnp.sum(jnp.exp(part - top), axis=0, keepdims=True) for part in logits)
@@ -338,8 +345,8 @@
             for number, part in zip(numbers, logits)
         )
         lse = top + jnp.log(total)
-        nllbuf[2 * k : 2 * k + 1, :] = jnp.where(left, lse, over(picked))
-        nllbuf[2 * k + 1 : 2 * k + 2, :] = jnp.where(left, over(lse), picked)
+        nllbuf[ends[0], :] = jnp.where(left, lse, over(picked))
+        nllbuf[ends[1], :] = jnp.where(left, over(lse), picked)
 
     def merged(buf, at, n):
         parts = [buf[at + k] for k in range(n)]
@@ -415,7 +422,7 @@
             pltpu.VMEM((NA * tok, kp), F32),
             pltpu.VMEM((PIECES, NZ, NB, NA * tok, kp), jnp.bfloat16),
             pltpu.VMEM((2, voc, width), jnp.bfloat16),
-            pltpu.VMEM((2, voc, tokens), F32),
+            pltpu.VMEM((2, 2, voc, tokens // 2), F32),
             pltpu.VMEM((NA * NB + NZ, 8, 128), F32),
             pltpu.VMEM((NA * NB + NZ, 8, 128), F32),
             pltpu.VMEM((2, 16, 128), F32),

time: 76.8 us -> 72.9 us (0.949)
  Pallas kernels: 73.7 us -> 69.8 us
    pallas_call x1, Pallas kernels: 73.7 us -> 69.8 us  [body(): pl.pallas_call(kernel, out_shape=jax.ShapeDtypeStruct((1, 128), F32), in_...]
where the time goes in v4:
time: 72.9 us; the launch traced here: 72.8 us
  Pallas kernels  69.8 us (96%)
  local copies, waits for them, and re-layouts  2.37 us (3%)
    pallas_call x1, Pallas kernels, body(): pl.pallas_call(kernel, out_shape=jax.ShapeDtypeStruct((1, 128), F32), in_...  69.8 us

profile of v4, /device:TPU:1, one launch (start us, length us, event | category | flops | bytes accessed | tf_op | source)
XLA Modules:
  0.0 72.8 jit_solution(16397193060211714231)
XLA Ops:
  0.6 69.8 %nll.1 = f32[1,128]{1,0:T(1,128)} custom-call(bf16[4,8192]{1,0:T(4,128)(2,1)} %hidden.1, bf16[501,8192]{1,0:T(8,128)(2,1)} %bitcast.7, s32[4]{0:T(128)} %targets.1, s32[4]{0:T(128)} %segment.1, s32[4]{0:T(128)} %pad_mask.1, s32[257]{0:T(512)} %seq_bench.1), custom_call_target="tpu_custom_call" | custom-call | tf_op jit(solution)/shard_map/nll/pallas_call | solution.py:411
  70.5 1.3 %slice_bitcast_fusion = (f32[8]{0:T(128)}, f32[8]{0:T(128)}) fusion(f32[1,128]{1,0:T(1,128)} %nll.1), kind=kLoop, calls=%fused_computation | loop fusion | bytes 128 | tf_op jit(solution)/shard_map/slice | solution.py:444
  71.7 1.1 %slice_bitcast_fusion.2 = f32[4]{0:T(128)} fusion(f32[1,128]{1,0:T(1,128)} %nll.1), kind=kLoop, calls=%fused_computation.2 | loop fusion | bytes 32 | tf_op jit(solution)/shard_map/slice | solution.py:444

commit v5 on v4

--- a/solution.py
+++ b/solution.py
@@ -11,15 +11,29 @@
 NBENCH = 8
 AXES = ("dp_0", "dp_1", "vocab_0", "vocab_1")
 NA, NB, NZ = 4, 4, 8
-PIECES = 8
-LAST = PIECES - 1
+PIECES = 3
+WIDE = 2304
+LAST = PIECES
 GROUP = NA * NB * NZ
-PLAN = {
-    (1, 3): [(0, 0)], (1, 5): [(1, 0)], (1, 6): [(2, 0)], (2, 0): [(3, 0)], (2, 3): [(0, 1)],
-    (3, 0): [(1, 1)], (3, 1): [(2, 1)], (3, 4): [(3, 1)],
-    (4, 1): [(0, 2), (1, 2)], (4, 2): [(2, 2)], (4, 3): [(3, 2)], (4, 5): [(0, 3)],
-    (4, 6): [(1, 3)], (4, 7): [(2, 3), (3, 3)], (4, 8): [(0, 4), (1, 4), (2, 4), (3, 4)],
-}
+PLAN = (
+    (
+        ("lv", 0, 1), ("ef", 0, 0), ("fw", 0, 0), ("fw", 1, 0), ("lv", 1, 1), ("fw", 2, 0),
+        ("lv", 2, 1), ("lv", 0, 2), ("fw", 0, 1), ("lv", 1, 2), ("fw", 1, 1), ("lv", 2, 2),
+        ("ez", 0, 0), ("ez", 1, 0), ("ef", 0, 1), ("ez", 2, 0), ("ez", 3, 0), ("fw", 2, 1),
+        ("lv", 0, 3), ("fw", 0, 2), ("lv", 1, 3), ("fw", 1, 2), ("lv", 2, 3), ("ez", 0, 1),
+        ("fw", 2, 2), ("ez", 1, 1), ("lv", 0, 4), ("ez", 2, 1),
+    ),
+    (("ez", 3, 1), ("fw", 0, 3), ("lv", 1, 4)),
+    (("ez", 0, 2), ("fw", 1, 3), ("lv", 2, 4)),
+    (
+        ("ez", 1, 2), ("fw", 2, 3), ("fw", 0, 4), ("fw", 1, 4), ("ez", 2, 2), ("fw", 2, 4),
+        ("ez", 3, 2), ("ez", 0, 3),
+    ),
+    (("ez", 1, 3),),
+    (("ez", 2, 3), ("ez", 3, 3)),
+    (("ez", 0, 4), ("ez", 1, 4)),
+    (("ez", 2, 4), ("ez", 3, 4)),
+)
 MESH = pl.DeviceIdType.MESH
 F32 = jnp.float32
 
@@ -28,8 +42,8 @@
     hidden, weights, targets, segment, pad_mask, seq_bench,
     out,
     tgt_s, seg_s, pad_s, ben_s,
-    abuf, rows32, gath, wbuf, acc, info, stat, last, nllbuf,
-    small, lsem, wlsem, wsend, wrecv, asend, arecv, zsend, zrecv,
+    abuf, ebuf, rows32, gath, egath, wbuf, acc, info, stat, last, nllbuf,
+    small, lsem, wlsem, wsend, wrecv, asend, easend, arecv, zsend, zrecv,
     bsend, brecv, fsend, frecv, ebsend, ebrecv, ezsend, ezrecv,
     isend, irecv, ssend, srecv, csend, crecv,
 ):
@@ -37,7 +51,7 @@
     z, y = lax.axis_index("vocab_0"), lax.axis_index("vocab_1")
     a = y * (1 - c) + x * c
     b = x * (1 - c) + y * c
-    kp = abuf.shape[3]
+    width = weights.shape[1]
     voc = weights.shape[0]
 
     def dev(a_, b_, z_):
@@ -61,10 +75,13 @@
     partner = (x, 1 - c, z, y)
 
     def columns(p):
-        return pl.ds(pl.multiple_of(p * kp, kp), kp)
+        return slice(p * WIDE, (p + 1) * WIDE if p < LAST else width)
+
+    def held(p):
+        return abuf.at[p] if p < LAST else ebuf
 
     def own_hidden(p):
-        return pltpu.make_async_copy(hidden.at[:, columns(p)], abuf.at[p, a], lsem.at[p])
+        return pltpu.make_async_copy(hidden.at[:, columns(p)], held(p).at[a], lsem.at[p])
 
     def own_weights(p):
         cols = columns(p)
@@ -77,10 +94,9 @@
     def loop(n, fn):
         lax.fori_loop(0, n, lambda i, _: (fn(i), 0)[1], 0)
 
-    def turn(i):
-        return lax.rem(i + LAST, PIECES)
-
-    loop(PIECES, lambda i: own_hidden(turn(i)).start())
+    turns = (LAST, *range(PIECES))
+    for p in turns:
+        own_hidden(p).start()
     smalls = [
         pltpu.make_async_copy(src, dst, small.at[k])
         for k, (src, dst) in enumerate(
@@ -100,17 +116,18 @@
     pl.semaphore_wait(barrier, len(peers))
 
     def a_copy(p, k):
-        return rdma(abuf.at[p, a], abuf.at[p, a], asend, arecv.at[p, k - 1], dev(a_at(k), b, z))
-
-    def a_start(i):
-        p = turn(i)
+        ssem = asend if p < LAST else easend
+        mine = held(p).at[a]
+        return rdma(mine, mine, ssem, arecv.at[p, k - 1], dev(a_at(k), b, z))
+
+    for p in turns:
         own_hidden(p).wait()
         for k in range(1, NA):
             a_copy(p, k).start()
-
-    loop(PIECES, a_start)
-    loop(PIECES, lambda p: own_weights(p).start())
-    loop(PIECES, lambda p: swap_weights(p).start())
+    for p in range(PIECES + 1):
+        own_weights(p).start()
+    for p in range(PIECES + 1):
+        swap_weights(p).start()
     acc[...] = jnp.zeros(acc.shape, F32)
 
     def planes(buf, ssem, rsem):
@@ -149,14 +166,15 @@
         return NZ - 1 - j // 2 if odd else j // 2
 
     def block(p, b_, z_):
-        return gath.at[p, z_, b_]
+        return egath.at[z_, b_] if p is LAST else gath.at[p, z_, b_]
 
     def z_copy(p, b_, k, ssem, rsem, up):
-        zi = z_at(k)
-        return rdma(block(p, b_, zi), block(p, b_, zi), ssem, rsem, dev(a, b, z_at(up)))
+        mine = block(p, b_, z_at(k))
+        return rdma(mine, mine, ssem, rsem, dev(a, b, z_at(up)))
 
     def b_send(p, zi, b_, ssem, rsem, go):
-        return rdma(block(p, b_, zi), block(p, b_, zi), ssem, rsem, dev(a, b_at(go), z))
+        mine = block(p, b_, zi)
+        return rdma(mine, mine, ssem, rsem, dev(a, b_at(go), z))
 
     def b_copy(p, j, way, odd=None):
         go = 1 if way == 0 else NB - 1
@@ -171,82 +189,91 @@
         b_copy(p, j, 0).start()
         b_copy(p, j, 1).start()
 
+    def e_copy(k, src, go):
+        return b_send(LAST, z, b_at(src), ebsend, ebrecv.at[k], go)
+
     def tile_rows(p):
+        wide = held(p).shape[2]
         for k in range(1, NA):
             a_copy(p, k).wait_recv()
         for k in range(NA):
-            rows32[4 * k : 4 * k + 4, :] = abuf[p, k].astype(F32)
-        gath[p, z, b] = rows32[...].astype(jnp.bfloat16)
-
-    def e_copy(k, src, go):
-        return b_send(LAST, z, b_at(src), ebsend, ebrecv.at[k], go)
-
-    tile_rows(LAST)
-    e_copy(0, 0, 1).start()
-    e_copy(1, 0, NB - 1).start()
-
-    def begin(p):
-        tile_rows(p)
-        b_both(p, 0)
-
-        z_step(p, 0, p, b, zsend, zrecv)
+            rows32[4 * k : 4 * k + 4, 0:wide] = held(p)[k].astype(F32)
+        tile = rows32[:, 0:wide].astype(jnp.bfloat16)
+        if p < LAST:
+            gath[p, z, b] = tile
+        else:
+            egath[z, b] = tile
 
     def z_step(p, s, u, b_, ssem, rsem):
+        odd = u % 2
         if s == 0:
             z_copy(p, b_, 0, ssem, rsem.at[u, 0], 1).start()
             z_copy(p, b_, 0, ssem, rsem.at[u, 1], NZ - 1).start()
         elif s < 4:
-            odd = lax.rem(u, 2)
             z_copy(p, b_, NZ - s, ssem, rsem.at[u, 2 * s - 2], 1).wait_recv()
             if s < 3:
                 z_copy(p, b_, NZ - s, ssem, rsem.at[u, 2 * s], 1).start()
+            elif not odd:
+                z_copy(p, b_, 5, ssem, rsem.at[u, 6], 1).start()
             z_copy(p, b_, s, ssem, rsem.at[u, 2 * s - 1], NZ - 1).wait_recv()
             if s < 3:
                 z_copy(p, b_, s, ssem, rsem.at[u, 2 * s + 1], NZ - 1).start()
-            else:
-                z_copy(p, b_, 5 + 6 * odd, ssem, rsem.at[u, 6], 1 + 6 * odd).start()
+            elif odd:
+                z_copy(p, b_, 3, ssem, rsem.at[u, 6], NZ - 1).start()
         else:
             z_copy(p, b_, 4, ssem, rsem.at[u, 6], 1).wait_recv()
 
-    loop(LAST, begin)
-
     def step(p, s):
         z_step(p, s, p, b, zsend, zrecv)
-        if 0 < s < 4:
+        if s == 0:
+            b_both(p, 0)
+        elif s < 4:
             b_both(p, 2 * s - 1)
             b_both(p, 2 * s)
-        elif s == 4:
+        else:
             b_both(p, 7)
 
     def e_step(u, s):
-        b_ = b_at(u + (u // 2) * (5 - 2 * u))
-        z_step(LAST, s, u, b_, ezsend, ezrecv)
+        z_step(LAST, s, u, b_at((0, 1, 3, 2)[u]), ezsend, ezrecv)
+
+    def e_along(_, s):
+        if s == 0:
+            e_copy(0, 0, 1).wait_recv()
+            e_copy(1, 0, NB - 1).wait_recv()
+            e_copy(2, NB - 1, 1).start()
+        else:
+            e_copy(2, NB - 1, 1).wait_recv()
 
     def forward(p, s):
         for j in ((0,), (1, 2), (3, 4), (5, 6), (7,))[s]:
             b_copy(p, j, j % 2).wait_recv()
             f_copy(p, j).start()
 
-    def multiply(p, h):
-        @pl.when(p < LAST)
-        def _():
-            for k in range(4):
-                b_copy(p, 4 * h + k, 1 - k % 2, k % 2).wait_recv()
-                f_copy(p, 4 * h + k, k % 2).wait_recv()
-
-        @pl.when(h == 0)
-        def _():
-            own_weights(p).wait()
-            swap_weights(p).wait_recv()
-
-        cols = columns(p)
+    def product(h, cols, wide, some):
         rows = jnp.concatenate(
-            [gath[p, z_at(dist(4 * h + k, k % 2))].reshape(NB * 16, kp) for k in range(4)], axis=0
+            [some(z_at(dist(4 * h + k, k % 2))).reshape(NB * 16, wide) for k in range(4)], axis=0
         )
         for w in range(2):
             acc[h, w] += lax.dot_general(
                 wbuf[w, :, cols], rows, (((1,), (1,)), ((), ())), preferred_element_type=F32
             )
+
+    def multiply(p, h):
+        for k in range(4):
+            b_copy(p, 4 * h + k, 1 - k % 2, k % 2).wait_recv()
+            f_copy(p, 4 * h + k, k % 2).wait_recv()
+        cols = pl.ds(pl.multiple_of(p * WIDE, WIDE), WIDE)
+        product(h, cols, WIDE, lambda zi: gath[p, zi])
+
+    def multiply_last(h):
+        product(h, columns(LAST), width - PIECES * WIDE, lambda zi: egath[zi])
+
+    tile_rows(LAST)
+    e_copy(0, 0, 1).start()
+    e_copy(1, 0, NB - 1).start()
+    for p in range(PIECES):
+        tile_rows(p)
+        step(p, 0)
 
     row = lax.broadcasted_iota(jnp.int32, (8, 128), 0)
     lane = lax.broadcasted_iota(jnp.int32, (8, 128), 1)
@@ -266,60 +293,38 @@
             own = jnp.where((row == z) & (lane == base + t + 64), code, own)
         return own.astype(F32)
 
-    def planned(s, i, count):
-        for at in range(count):
-            if (s, at) in PLAN:
-
-                @pl.when(i == at)
-                def _():
-                    for u, k in PLAN[s, at]:
-                        e_step(u, k)
-
-    def level(s, p):
-        if s == 1:
-
-            @pl.when(p == 0)
+    handle = {"lv": step, "fw": forward, "ez": e_step, "ef": e_along}
+
+    def slot(i):
+        for k, things in enumerate(PLAN):
+
+            @pl.when(i == k)
             def _():
-                e_copy(0, 0, 1).wait_recv()
-                e_copy(1, 0, NB - 1).wait_recv()
-                e_copy(2, NB - 1, 1).start()
-
-            @pl.when(p == 6)
-            def _():
-                e_copy(2, NB - 1, 1).wait_recv()
-
-        planned(s, p, LAST)
-        step(p, s)
-        forward(p, s - 1)
-
-    for s in range(1, 4):
-        loop(LAST, functools.partial(level, s))
-
-    def finish(i):
-        planned(4, i, PIECES + 1)
-
-        @pl.when(i < LAST)
+                for what, which, s in things:
+                    handle[what](which, s)
+                if k < PIECES + 1:
+                    own_weights(k).wait()
+                    swap_weights(k).wait_recv()
+                if k == 1:
+                    wait_all(smalls)
+                    info[a * NB + b] = own_info()
+                    start_all(planes(info, isend, irecv))
+                if k == 5:
+                    wait_all(planes(info, isend, irecv))
+                    info[NA * NB + z] = added(info, 0, NA * NB)
+                    start_all(lines(info, isend, irecv))
+
+        p, h = lax.rem(i, PIECES + 1), i // (PIECES + 1)
+
+        @pl.when(p < LAST)
         def _():
-            step(i, 4)
-            forward(i, 3)
-
-        @pl.when(i == 1)
+            multiply(p, h)
+
+        @pl.when(p == LAST)
         def _():
-            wait_all(smalls)
-            info[a * NB + b] = own_info()
-            start_all(planes(info, isend, irecv))
-
-        @pl.when(i == LAST)
-        def _():
-            loop(LAST, lambda p: forward(p, 4))
-            wait_all(planes(info, isend, irecv))
-            info[NA * NB + z] = added(info, 0, NA * NB)
-            start_all(lines(info, isend, irecv))
-
-        h = i // PIECES
-        multiply(lax.rem(i + h * LAST, PIECES), h)
-
-    loop(2 * PIECES, finish)
+            multiply_last(h)
+
+    loop(len(PLAN), slot)
     wait_all(lines(info, isend, irecv))
     info[0] = added(info, NA * NB, NZ)
 
@@ -385,12 +390,13 @@
         rdma(ref, ref, ssem, rsem, partner).wait_send()
 
     left_all(abuf.at[:, 0:3], asend, arecv.at[0, 0])
+    left_all(ebuf.at[0:3], easend, arecv.at[0, 0])
     rdma(weights, wbuf.at[1], wsend, wrecv.at[0], partner).wait_send()
-    left_all(gath.at[0:LAST, 0:7, 0], zsend, zrecv.at[0, 0])
-    left_all(gath.at[0:LAST, 0:4], bsend, brecv.at[0, 0, 0])
-    left_all(gath.at[0:LAST, 0:2], fsend, frecv.at[0, 0])
-    left_all(gath.at[LAST, 0, 0:3], ebsend, ebrecv.at[0])
-    left_all(gath.at[LAST, 0:7], ezsend, ezrecv.at[0, 0])
+    left_all(gath.at[:, 0:7, 0], zsend, zrecv.at[0, 0])
+    left_all(gath.at[:, 0:4], bsend, brecv.at[0, 0, 0])
+    left_all(gath.at[:, 0:2], fsend, frecv.at[0, 0])
+    left_all(egath.at[0, 0:3], ebsend, ebrecv.at[0])
+    left_all(egath.at[0:7], ezsend, ezrecv.at[0, 0])
 
     swap.wait()
     sums = jnp.sum(last[0] + last[1], axis=1, keepdims=True)
@@ -403,7 +409,7 @@
 def body(hidden, lm_head, targets, segment, pad_mask, seq_bench):
     tok, width = hidden.shape
     voc = lm_head.shape[1]
-    kp = width // PIECES
+    rest = width - PIECES * WIDE
     tokens = GROUP * tok
     dma = pltpu.SemaphoreType.DMA
     anywhere = pl.BlockSpec(memory_space=pl.ANY)
@@ -418,18 +424,20 @@
             pltpu.SMEM((tok,), jnp.int32),
             pltpu.SMEM((tok,), jnp.int32),
             pltpu.SMEM(seq_bench.shape, jnp.int32),
-            pltpu.VMEM((PIECES, NA, tok, kp), jnp.bfloat16),
-            pltpu.VMEM((NA * tok, kp), F32),
-            pltpu.VMEM((PIECES, NZ, NB, NA * tok, kp), jnp.bfloat16),
+            pltpu.VMEM((PIECES, NA, tok, WIDE), jnp.bfloat16),
+            pltpu.VMEM((NA, tok, rest), jnp.bfloat16),
+            pltpu.VMEM((NA * tok, WIDE), F32),
+            pltpu.VMEM((PIECES, NZ, NB, NA * tok, WIDE), jnp.bfloat16),
+            pltpu.VMEM((NZ, NB, NA * tok, rest), jnp.bfloat16),
             pltpu.VMEM((2, voc, width), jnp.bfloat16),
             pltpu.VMEM((2, 2, voc, tokens // 2), F32),
             pltpu.VMEM((NA * NB + NZ, 8, 128), F32),
             pltpu.VMEM((NA * NB + NZ, 8, 128), F32),
             pltpu.VMEM((2, 16, 128), F32),
             pltpu.VMEM((8, 128), F32),
-            dma((4,)), dma((PIECES,)), dma((PIECES,)), dma, dma((PIECES,)),
-            dma, dma((PIECES, NA - 1)), dma, dma((LAST, NZ - 1)),
-            dma, dma((LAST, 2, NZ)), dma, dma((LAST, NZ)),
+            dma((4,)), dma((PIECES + 1,)), dma((PIECES + 1,)), dma, dma((PIECES + 1,)),
+            dma, dma, dma((PIECES + 1, NA - 1)), dma, dma((PIECES, NZ - 1)),
+            dma, dma((PIECES, 2, NZ)), dma, dma((PIECES, NZ)),
             dma, dma((3,)), dma, dma((NB, NZ - 1)),
             dma((NA * NB + NZ,)), dma((NA * NB + NZ,)),
             dma((NA * NB + NZ,)), dma((NA * NB + NZ,)),
@@ -440,8 +448,22 @@
         ),
         name="nll",
     )(hidden, lm_head.T, targets, segment, pad_mask, seq_bench)
-    line = out[0]
-    return (line[:tok], line[tok : tok + NBENCH], line[tok + NBENCH : tok + 2 * NBENCH])
+
+    def split(line, first, second, third):
+        first[...] = line[:, 0:tok]
+        second[...] = line[:, tok : tok + NBENCH]
+        third[...] = line[:, tok + NBENCH : tok + 2 * NBENCH]
+
+    nll, total, count = pl.pallas_call(
+        split,
+        out_shape=(
+            jax.ShapeDtypeStruct((1, tok), F32),
+            jax.ShapeDtypeStruct((1, NBENCH), F32),
+            jax.ShapeDtypeStruct((1, NBENCH), F32),
+        ),
+        name="split",
+    )(out)
+    return (nll.reshape(tok), total.reshape(NBENCH), count.reshape(NBENCH))
 
 
 def solution(mesh):

time: 72.9 us -> 69.7 us (0.956)
  local copies, waits for them, and re-layouts: 2.37 us -> 0 us
  Pallas kernels: 69.8 us -> 69 us
    slice x2 -> x0, local copies, waits for them, and re-layouts: 2.37 us -> none  [the longest x1 1.26 us: body(): line[tok + NBENCH:tok + 2 * NBENCH]]
    pallas_call x1, Pallas kernels: 69.8 us -> 67.8 us  [body(): pl.pallas_call(kernel, out_shape=jax.ShapeDtypeStruct((1, 128), F32), in_...]
    pallas_call x0 -> x1, Pallas kernels: none -> 1.18 us  [body(): pl.pallas_call(split, out_shape=(jax.ShapeDtypeStruct((1, tok), F32), jax...]
where the time goes in v5:
time: 69.7 us; the launch traced here: 69.6 us
  Pallas kernels  69 us (99%)
    pallas_call x1, Pallas kernels, body(): pl.pallas_call(kernel, out_shape=jax.ShapeDtypeStruct((1, 128), F32), in_...  67.8 us

profile of v5, /device:TPU:1, one launch (start us, length us, event | category | flops | bytes accessed | tf_op | source)
XLA Modules:
  0.0 69.6 jit_solution(1554399626729561099)
XLA Ops:
  0.6 67.8 %nll.1.line = f32[1,128]{1,0:T(1,128)} custom-call(bf16[4,8192]{1,0:T(4,128)(2,1)} %hidden.1, bf16[501,8192]{1,0:T(8,128)(2,1)} %bitcast.4, s32[4]{0:T(128)} %targets.1, s32[4]{0:T(128)} %segment.1, s32[4]{0:T(128)} %pad_mask.1, s32[257]{0:T(512)} %seq_bench.1), custom_call_target="tpu_custom_call" | custom-call | tf_op jit(solution)/shard_map/nll/pallas_call | solution.py:417
  68.4 1.2 %split.1 = (f32[1,4]{1,0:T(1,128)}, f32[1,8]{1,0:T(1,128)}, f32[1,8]{1,0:T(1,128)}) custom-call(f32[1,128]{1,0:T(1,128)} %nll.1.line), custom_call_target="tpu_custom_call" | custom-call | tf_op jit(solution)/shard_map/split/pallas_call | solution.py:457

commit v6 on v5

--- a/solution.py
+++ b/solution.py
@@ -19,9 +19,10 @@
     (
         ("lv", 0, 1), ("ef", 0, 0), ("fw", 0, 0), ("fw", 1, 0), ("lv", 1, 1), ("fw", 2, 0),
         ("lv", 2, 1), ("lv", 0, 2), ("fw", 0, 1), ("lv", 1, 2), ("fw", 1, 1), ("lv", 2, 2),
-        ("ez", 0, 0), ("ez", 1, 0), ("ef", 0, 1), ("ez", 2, 0), ("ez", 3, 0), ("fw", 2, 1),
+        ("ez", 0, 0), ("ez", 1, 0), ("ef", 0, 1), ("in", 0, 0), ("ez", 2, 0), ("ez", 3, 0), ("fw", 2, 1),
         ("lv", 0, 3), ("fw", 0, 2), ("lv", 1, 3), ("fw", 1, 2), ("lv", 2, 3), ("ez", 0, 1),
-        ("fw", 2, 2), ("ez", 1, 1), ("lv", 0, 4), ("ez", 2, 1),
+        ("fw", 2, 2), ("ez", 1, 1), ("lv", 0, 4), ("in", 0, 1),
+        ("ez", 2, 1),
     ),
     (("ez", 3, 1), ("fw", 0, 3), ("lv", 1, 4)),
     (("ez", 0, 2), ("fw", 1, 3), ("lv", 2, 4)),
@@ -29,7 +30,7 @@
         ("ez", 1, 2), ("fw", 2, 3), ("fw", 0, 4), ("fw", 1, 4), ("ez", 2, 2), ("fw", 2, 4),
         ("ez", 3, 2), ("ez", 0, 3),
     ),
-    (("ez", 1, 3),),
+    (("in", 0, 2), ("ez", 1, 3)),
     (("ez", 2, 3), ("ez", 3, 3)),
     (("ez", 0, 4), ("ez", 1, 4)),
     (("ez", 2, 4), ("ez", 3, 4)),
@@ -42,10 +43,10 @@
     hidden, weights, targets, segment, pad_mask, seq_bench,
     out,
     tgt_s, seg_s, pad_s, ben_s,
-    abuf, ebuf, rows32, gath, egath, wbuf, acc, info, stat, last, nllbuf,
+    abuf, ebuf, rows32, gath, egath, wbuf, acc, info, stat, xinfo, xstat, nllbuf,
     small, lsem, wlsem, wsend, wrecv, asend, easend, arecv, zsend, zrecv,
     bsend, brecv, fsend, frecv, ebsend, ebrecv, ezsend, ezrecv,
-    isend, irecv, ssend, srecv, csend, crecv,
+    isend, irecv, ssend, srecv, xisend, xirecv, xssend, xsrecv,
 ):
     x, c = lax.axis_index("dp_0"), lax.axis_index("dp_1")
     z, y = lax.axis_index("vocab_0"), lax.axis_index("vocab_1")
@@ -145,6 +146,14 @@
                 dev(a, b, z_at(k)),
             )
             for k in range(1, NZ)
+        ]
+
+    def crossings(buf, far, ssem, rsem):
+        return [
+            rdma(
+                buf.at[NA * NB + z], far.at[z], ssem.at[k], rsem.at[k], (x, 1 - c, z_at(k), y)
+            )
+            for k in range(NZ)
         ]
 
     def start_all(copies):
@@ -289,11 +298,51 @@
             else:
                 kept = (pad_s[t] == 1) & jnp.logical_not(whole_last)
             code = jnp.where(kept, ben_s[seg], NBENCH)
-            own = jnp.where((row == z) & (lane == base + t), tgt_s[t], own)
-            own = jnp.where((row == z) & (lane == base + t + 64), code, own)
+            own = jnp.where(lane == base + t, tgt_s[t], own)
+            own = jnp.where(lane == base + t + 64, code, own)
         return own.astype(F32)
 
-    handle = {"lv": step, "fw": forward, "ez": e_step, "ef": e_along}
+    def along_info(_, s):
+        if s == 0:
+            wait_all(smalls)
+            info[a * NB + b] = own_info()[0:1]
+            start_all(planes(info, isend, irecv))
+        elif s == 1:
+            wait_all(planes(info, isend, irecv))
+            info[NA * NB + z] = added(info, 0, NA * NB)
+            start_all(lines(info, isend, irecv))
+            start_all(crossings(info, xinfo, xisend, xirecv))
+        else:
+            wait_all(lines(info, isend, irecv))
+            wait_all(crossings(info, xinfo, xisend, xirecv))
+
+    index = ((x * 2 + c) * NZ + z) * NB + y
+    other = ((x * 2 + 1 - c) * NZ + z) * NB + y
+    entries = lax.broadcasted_iota(jnp.int32, (voc, 128), 0)
+    numbers = [(entries + i * voc).astype(F32) for i in (index, other)]
+    left = lane[0:1, :] < 64
+
+    def over(line):
+        return pltpu.roll(jnp.broadcast_to(line, (8, 128)), 64, 1)[0:1, :]
+
+    def statistics(h):
+        for k in (2 * h, 2 * h + 1):
+            near = [z_at(dist(2 * k + m)) for m in range(2)]
+            ends = [pl.ds(zi, 1) for zi in near]
+            logits = [acc[k // 2, w, :, (k % 2) * 128 : (k % 2 + 1) * 128] for w in range(2)]
+            wanted = jnp.where(left, info[NA * NB + near[0]], over(info[NA * NB + near[1]]))
+            tops = [jnp.max(part, axis=0, keepdims=True) for part in logits]
+            top = jnp.maximum(*tops)
+            total = sum(jnp.sum(jnp.exp(part - top), axis=0, keepdims=True) for part in logits)
+            picked = sum(
+                jnp.sum(jnp.where(number == wanted, part, 0.0), axis=0, keepdims=True)
+                for number, part in zip(numbers, logits)
+            )
+            lse = top + jnp.log(total)
+            nllbuf[ends[0], :] = jnp.where(left, lse, over(picked))
+            nllbuf[ends[1], :] = jnp.where(left, over(lse), picked)
+
+    handle = {"lv": step, "fw": forward, "ez": e_step, "ef": e_along, "in": along_info}
 
     def slot(i):
         for k, things in enumerate(PLAN):
@@ -305,14 +354,8 @@
                 if k < PIECES + 1:
                     own_weights(k).wait()
                     swap_weights(k).wait_recv()
-                if k == 1:
-                    wait_all(smalls)
-                    info[a * NB + b] = own_info()
-                    start_all(planes(info, isend, irecv))
-                if k == 5:
-                    wait_all(planes(info, isend, irecv))
-                    info[NA * NB + z] = added(info, 0, NA * NB)
-                    start_all(lines(info, isend, irecv))
+                if k == 6:
+                    statistics(0)
 
         p, h = lax.rem(i, PIECES + 1), i // (PIECES + 1)
 
@@ -325,34 +368,7 @@
             multiply_last(h)
 
     loop(len(PLAN), slot)
-    wait_all(lines(info, isend, irecv))
-    info[0] = added(info, NA * NB, NZ)
-
-    index = ((x * 2 + c) * NZ + z) * NB + y
-    other = ((x * 2 + 1 - c) * NZ + z) * NB + y
-    entries = lax.broadcasted_iota(jnp.int32, (voc, 128), 0)
-    numbers = [(entries + i * voc).astype(F32) for i in (index, other)]
-    left = lane[0:1, :] < 64
-    every = info[0]
-
-    def over(line):
-        return pltpu.roll(jnp.broadcast_to(line, (8, 128)), 64, 1)[0:1, :]
-
-    for k in range(4):
-        ends = [pl.ds(z_at(dist(2 * k + m)), 1) for m in range(2)]
-        logits = [acc[k // 2, w, :, (k % 2) * 128 : (k % 2 + 1) * 128] for w in range(2)]
-        wanted = jnp.where(left, info[0, ends[0], :], over(info[0, ends[1], :]))
-        tops = [jnp.max(part, axis=0, keepdims=True) for part in logits]
-        top = jnp.maximum(*tops)
-        total = sum(jnp.sum(jnp.exp(part - top), axis=0, keepdims=True) for part in logits)
-        picked = sum(
-            jnp.sum(jnp.where(number == wanted, part, 0.0), axis=0, keepdims=True)
-            for number, part in zip(numbers, logits)
-        )
-        lse = top + jnp.log(total)
-        nllbuf[ends[0], :] = jnp.where(left, lse, over(picked))
-        nllbuf[ends[1], :] = jnp.where(left, over(lse), picked)
-
+    statistics(1)
     def merged(buf, at, n):
         parts = [buf[at + k] for k in range(n)]
         top = functools.reduce(jnp.maximum, parts)
@@ -365,27 +381,7 @@
     wait_all(planes(stat, ssend, srecv))
     stat[NA * NB + z] = merged(stat, 0, NA * NB)
     start_all(lines(stat, ssend, srecv))
-    wait_all(lines(stat, ssend, srecv))
-    both = merged(stat, NA * NB, NZ)
-    nll = both - pltpu.roll(both, 64, 1)
-
-    codes = jnp.where(lane < 64, pltpu.roll(every, 64, 1), float(NBENCH))
-    last_t, last_c = jnp.zeros((8, 128), F32), jnp.zeros((8, 128), F32)
-    for j in range(NBENCH):
-        hit = codes == float(j)
-        part_t = jnp.sum(jnp.where(hit, nll, 0.0), axis=0, keepdims=True)
-        part_c = jnp.sum(jnp.where(hit, 1.0, 0.0), axis=0, keepdims=True)
-        last_t = jnp.where(row == j, part_t, last_t)
-        last_c = jnp.where(row == j, part_c, last_c)
-    last[c, 0:8, :] = last_t
-    last[c, 8:16, :] = last_c
-    swap = rdma(last.at[c], last.at[c], csend, crecv, partner)
-    swap.start()
-
-    nllbuf[...] = nll
-    mine = nllbuf[pl.ds(z, 1), :]
-    rolled = pltpu.roll(jnp.broadcast_to(mine, (8, 128)), lax.rem(128 - base, 128), 1)
-
+    start_all(crossings(stat, xstat, xssend, xsrecv))
     def left_all(ref, ssem, rsem):
         rdma(ref, ref, ssem, rsem, partner).wait_send()
 
@@ -398,8 +394,35 @@
     left_all(egath.at[0, 0:3], ebsend, ebrecv.at[0])
     left_all(egath.at[0:7], ezsend, ezrecv.at[0, 0])
 
-    swap.wait()
-    sums = jnp.sum(last[0] + last[1], axis=1, keepdims=True)
+    def losses(buf, at):
+        both = merged(buf, at, NZ)
+        return both - pltpu.roll(both, 64, 1)
+
+    def gathered(buf, at):
+        return jnp.concatenate([buf[at + k] for k in range(NZ)], axis=0)
+
+    def by_core(mine, others, first, second):
+        lower, upper = jnp.where(c == 0, mine, others), jnp.where(c == 0, others, mine)
+        lower = pltpu.roll(lower, 64, 1) if first else lower
+        upper = pltpu.roll(upper, 64, 1) if second else upper
+        return jnp.where(lane < 64, lower, upper)
+
+    codes = by_core(gathered(info, NA * NB), gathered(xinfo, 0), True, False)
+    wait_all(lines(stat, ssend, srecv))
+    nll = losses(stat, NA * NB)
+    nllbuf[...] = nll
+    mine = nllbuf[pl.ds(z, 1), :]
+    rolled = pltpu.roll(jnp.broadcast_to(mine, (8, 128)), lax.rem(128 - base, 128), 1)
+    wait_all(crossings(stat, xstat, xssend, xsrecv))
+    loss = by_core(nll, losses(xstat, 0), False, True)
+    last_t, last_c = jnp.zeros((8, 128), F32), jnp.zeros((8, 128), F32)
+    for j in range(NBENCH):
+        hit = codes == float(j)
+        part_t = jnp.sum(jnp.where(hit, loss, 0.0), axis=0, keepdims=True)
+        part_c = jnp.sum(jnp.where(hit, 1.0, 0.0), axis=0, keepdims=True)
+        last_t = jnp.where(row == j, part_t, last_t)
+        last_c = jnp.where(row == j, part_c, last_c)
+    sums = jnp.sum(jnp.concatenate([last_t, last_c], axis=0), axis=1, keepdims=True)
     row16 = lax.broadcasted_iota(jnp.int32, (16, 128), 0)
     lane16 = lax.broadcasted_iota(jnp.int32, (16, 128), 1)
     sums = jnp.sum(jnp.where(lane16 == row16 + 4, sums, 0.0), axis=0, keepdims=True)
@@ -431,9 +454,10 @@
             pltpu.VMEM((NZ, NB, NA * tok, rest), jnp.bfloat16),
             pltpu.VMEM((2, voc, width), jnp.bfloat16),
             pltpu.VMEM((2, 2, voc, tokens // 2), F32),
+            pltpu.VMEM((NA * NB + NZ, 1, 128), F32),
             pltpu.VMEM((NA * NB + NZ, 8, 128), F32),
-            pltpu.VMEM((NA * NB + NZ, 8, 128), F32),
-            pltpu.VMEM((2, 16, 128), F32),
+            pltpu.VMEM((NZ, 1, 128), F32),
+            pltpu.VMEM((NZ, 8, 128), F32),
             pltpu.VMEM((8, 128), F32),
             dma((4,)), dma((PIECES + 1,)), dma((PIECES + 1,)), dma, dma((PIECES + 1,)),
             dma, dma, dma((PIECES + 1, NA - 1)), dma, dma((PIECES, NZ - 1)),
@@ -441,7 +465,7 @@
             dma, dma((3,)), dma, dma((NB, NZ - 1)),
             dma((NA * NB + NZ,)), dma((NA * NB + NZ,)),
             dma((NA * NB + NZ,)), dma((NA * NB + NZ,)),
-            dma, dma,
+            dma((NZ,)), dma((NZ,)), dma((NZ,)), dma((NZ,)),
         ],
         compiler_params=pltpu.CompilerParams(
             collective_id=0, has_side_effects=True, vmem_limit_bytes=62 * 1024 * 1024

time: 69.7 us -> 67.9 us (0.974)
  Pallas kernels: 69 us -> 67.2 us
    pallas_call x1, Pallas kernels: 67.8 us -> 66 us  [body(): pl.pallas_call(kernel, out_shape=jax.ShapeDtypeStruct((1, 128), F32), in_...]
where the time goes in v6:
time: 67.9 us
  Pallas kernels  67.2 us (99%)
    pallas_call x1, Pallas kernels, body(): pl.pallas_call(kernel, out_shape=jax.ShapeDtypeStruct((1, 128), F32), in_...  66 us

profile of v6, /device:TPU:1, one launch (start us, length us, event | category | flops | bytes accessed | tf_op | source)
XLA Modules:
  0.0 67.9 jit_solution(11649507414962481513)
XLA Ops:
  0.6 66.0 %nll.1.line = f32[1,128]{1,0:T(1,128)} custom-call(bf16[4,8192]{1,0:T(4,128)(2,1)} %hidden.1, bf16[501,8192]{1,0:T(8,128)(2,1)} %bitcast.4, s32[4]{0:T(128)} %targets.1, s32[4]{0:T(128)} %segment.1, s32[4]{0:T(128)} %pad_mask.1, s32[257]{0:T(512)} %seq_bench.1), custom_call_target="tpu_custom_call" | custom-call | tf_op jit(solution)/shard_map/nll/pallas_call | solution.py:440
  66.7 1.2 %split.1 = (f32[1,4]{1,0:T(1,128)}, f32[1,8]{1,0:T(1,128)}, f32[1,8]{1,0:T(1,128)}) custom-call(f32[1,128]{1,0:T(1,128)} %nll.1.line), custom_call_target="tpu_custom_call" | custom-call | tf_op jit(solution)/shard_map/split/pallas_call | solution.py:481

commit v7 on v6

--- a/solution.py
+++ b/solution.py
@@ -17,23 +17,21 @@
 GROUP = NA * NB * NZ
 PLAN = (
     (
-        ("lv", 0, 1), ("ef", 0, 0), ("fw", 0, 0), ("fw", 1, 0), ("lv", 1, 1), ("fw", 2, 0),
-        ("lv", 2, 1), ("lv", 0, 2), ("fw", 0, 1), ("lv", 1, 2), ("fw", 1, 1), ("lv", 2, 2),
-        ("ez", 0, 0), ("ez", 1, 0), ("ef", 0, 1), ("in", 0, 0), ("ez", 2, 0), ("ez", 3, 0), ("fw", 2, 1),
-        ("lv", 0, 3), ("fw", 0, 2), ("lv", 1, 3), ("fw", 1, 2), ("lv", 2, 3), ("ez", 0, 1),
-        ("fw", 2, 2), ("ez", 1, 1), ("lv", 0, 4), ("in", 0, 1),
-        ("ez", 2, 1),
+        ("ef", 0, 0), ("fw", 0, 0), ("lv", 0, 1), ("lv", 1, 1), ("lv", 2, 1), ("lv", 0, 2),
+        ("fw", 1, 0), ("lv", 1, 2), ("ef", 0, 1), ("in", 0, 0), ("ez", 3, 0), ("lv", 2, 2),
+        ("fw", 2, 1), ("fw", 0, 1), ("fw", 0, 2), ("ez", 2, 0), ("fw", 1, 1), ("lv", 0, 3),
+        ("ez", 1, 0), ("ez", 0, 0), ("fw", 2, 0), ("ez", 3, 1), ("fw", 1, 2), ("fw", 2, 2),
+        ("ez", 2, 1), ("lv", 1, 3), ("lv", 0, 4), ("in", 0, 1), ("lv", 2, 3),
     ),
-    (("ez", 3, 1), ("fw", 0, 3), ("lv", 1, 4)),
-    (("ez", 0, 2), ("fw", 1, 3), ("lv", 2, 4)),
+    (("ez", 1, 1), ("ez", 0, 1)),
+    (("ez", 3, 2), ("fw", 0, 3), ("ez", 2, 2), ("lv", 1, 4)),
     (
-        ("ez", 1, 2), ("fw", 2, 3), ("fw", 0, 4), ("fw", 1, 4), ("ez", 2, 2), ("fw", 2, 4),
-        ("ez", 3, 2), ("ez", 0, 3),
+        ("lv", 2, 4), ("fw", 0, 4), ("ez", 1, 2), ("fw", 1, 3), ("ez", 0, 2), ("fw", 1, 4),
     ),
-    (("in", 0, 2), ("ez", 1, 3)),
-    (("ez", 2, 3), ("ez", 3, 3)),
-    (("ez", 0, 4), ("ez", 1, 4)),
-    (("ez", 2, 4), ("ez", 3, 4)),
+    (("fw", 2, 3), ("ez", 2, 3), ("fw", 2, 4), ("ez", 3, 3)),
+    (("ez", 1, 3), ("ez", 0, 3), ("in", 0, 2)),
+    (("ez", 3, 4), ("ez", 2, 4)),
+    (("ez", 1, 4), ("ez", 0, 4)),
 )
 MESH = pl.DeviceIdType.MESH
 F32 = jnp.float32

time: 67.9 us -> 65.8 us (0.969)
  Pallas kernels: 67.2 us -> 65.1 us
    pallas_call x1, Pallas kernels: 66 us -> 63.9 us  [body(): pl.pallas_call(kernel, out_shape=jax.ShapeDtypeStruct((1, 128), F32), in_...]
where the time goes in v7:
time: 65.8 us
  Pallas kernels  65.1 us (99%)
    pallas_call x1, Pallas kernels, body(): pl.pallas_call(kernel, out_shape=jax.ShapeDtypeStruct((1, 128), F32), in_...  63.9 us

profile of v7, /device:TPU:1, one launch (start us, length us, event | category | flops | bytes accessed | tf_op | source)
XLA Modules:
  0.0 65.8 jit_solution(15230336684263660681)
XLA Ops:
  0.6 63.9 %nll.1.line = f32[1,128]{1,0:T(1,128)} custom-call(bf16[4,8192]{1,0:T(4,128)(2,1)} %hidden.1, bf16[501,8192]{1,0:T(8,128)(2,1)} %bitcast.4, s32[4]{0:T(128)} %targets.1, s32[4]{0:T(128)} %segment.1, s32[4]{0:T(128)} %pad_mask.1, s32[257]{0:T(512)} %seq_bench.1), custom_call_target="tpu_custom_call" | custom-call | tf_op jit(solution)/shard_map/nll/pallas_call | solution.py:438
  64.6 1.2 %split.1 = (f32[1,4]{1,0:T(1,128)}, f32[1,8]{1,0:T(1,128)}, f32[1,8]{1,0:T(1,128)}) custom-call(f32[1,128]{1,0:T(1,128)} %nll.1.line), custom_call_target="tpu_custom_call" | custom-call | tf_op jit(solution)/shard_map/split/pallas_call | solution.py:479

commit v8 on v7

--- a/solution.py
+++ b/solution.py
@@ -33,6 +33,8 @@
     (("ez", 3, 4), ("ez", 2, 4)),
     (("ez", 1, 4), ("ez", 0, 4)),
 )
+FAR_PLANE = (10, 2, 8, 6, 9, 11, 14, 1, 3, 4, 12, 5, 7, 13, 15)
+FAR_LINE = (4, 3, 5, 2, 6, 1, 7)
 MESH = pl.DeviceIdType.MESH
 F32 = jnp.float32
 
@@ -133,7 +135,7 @@
         at = a * NB + b
         return [
             rdma(buf.at[at], buf.at[at], ssem.at[k], rsem.at[k], dev(a_at(k // NB), b_at(k % NB), z))
-            for k in range(1, NA * NB)
+            for k in FAR_PLANE
         ]
 
     def lines(buf, ssem, rsem):
@@ -143,7 +145,7 @@
                 buf.at[at], buf.at[at], ssem.at[NA * NB + k], rsem.at[NA * NB + k],
                 dev(a, b, z_at(k)),
             )
-            for k in range(1, NZ)
+            for k in FAR_LINE
         ]
 
     def crossings(buf, far, ssem, rsem):
@@ -151,7 +153,7 @@
             rdma(
                 buf.at[NA * NB + z], far.at[z], ssem.at[k], rsem.at[k], (x, 1 - c, z_at(k), y)
             )
-            for k in range(NZ)
+            for k in (*FAR_LINE, 0)
         ]
 
     def start_all(copies):
@@ -378,8 +380,8 @@
     start_all(planes(stat, ssend, srecv))
     wait_all(planes(stat, ssend, srecv))
     stat[NA * NB + z] = merged(stat, 0, NA * NB)
+    start_all(crossings(stat, xstat, xssend, xsrecv))
     start_all(lines(stat, ssend, srecv))
-    start_all(crossings(stat, xstat, xssend, xsrecv))
     def left_all(ref, ssem, rsem):
         rdma(ref, ref, ssem, rsem, partner).wait_send()
 

time: 65.8 us -> 65.2 us (level)
  no operation moved by 1% of the time
where the time goes in v8:
time: 65.2 us; the launch traced here: 65.1 us
  Pallas kernels  64.5 us (99%)
    pallas_call x1, Pallas kernels, body(): pl.pallas_call(kernel, out_shape=jax.ShapeDtypeStruct((1, 128), F32), in_...  63.3 us

profile of v8, /device:TPU:1, one launch (start us, length us, event | category | flops | bytes accessed | tf_op | source)
XLA Modules:
  0.0 65.1 jit_solution(10909328123259950960)
XLA Ops:
  0.6 63.3 %nll.1.line = f32[1,128]{1,0:T(1,128)} custom-call(bf16[4,8192]{1,0:T(4,128)(2,1)} %hidden.1, bf16[501,8192]{1,0:T(8,128)(2,1)} %bitcast.4, s32[4]{0:T(128)} %targets.1, s32[4]{0:T(128)} %segment.1, s32[4]{0:T(128)} %pad_mask.1, s32[257]{0:T(512)} %seq_bench.1), custom_call_target="tpu_custom_call" | custom-call | tf_op jit(solution)/shard_map/nll/pallas_call | solution.py:440
  64.0 1.2 %split.1 = (f32[1,4]{1,0:T(1,128)}, f32[1,8]{1,0:T(1,128)}, f32[1,8]{1,0:T(1,128)}) custom-call(f32[1,128]{1,0:T(1,128)} %nll.1.line), custom_call_target="tpu_custom_call" | custom-call | tf_op jit(solution)/shard_map/split/pallas_call | solution.py:481
